TPU v7x, 128 devices: a whole 4x4x4 slice. The times are simulated.
128 devices in a mesh: ctx: 16 (over y_hi, z, core), vocab: 8 (over x, y_lo).
Axes of the slice: x: 4, y: 4 (y_hi: 2, y_lo: 2; y = y_hi * 2 + y_lo), z: 4, core: 2. Of those that a mesh axis runs over, the one named last changes fastest.
Arguments:
- hidden_in: bfloat16 [2048, 4096], P('ctx'), may hold values from -128 to 128
- attn_gain: float32 [4096], replicated, may hold values from 0.1 to 1.9
- w_query: bfloat16 [4096, 4096], P(None, 'vocab'), may hold values from -2 to 2
- w_key: bfloat16 [4096, 1024], P(None, 'vocab'), may hold values from -2 to 2
- w_value: bfloat16 [4096, 1024], P(None, 'vocab'), may hold values from -0.09375 to 0.09375
- w_out: bfloat16 [4096, 4096], P('vocab'), may hold values from -0.5 to 0.5
- final_gain: float32 [4096], replicated, may hold values from 0.5 to 1.5
- teacher_head: bfloat16 [65536, 4096], P(('vocab', 'ctx')), may hold values from -18 to 18
- draft_rows: bfloat16 [2048, 2048], P('ctx'), may hold values from -1.5 to 1.5
- draft_head: bfloat16 [65536, 2048], P(('vocab', 'ctx')), may hold values from -64 to 64
- target_ids: int32 [2048], replicated, may hold values from 0 to 65535
- rollout_lengths: int32 [4], replicated, may hold values from 1 to 1024, 2048 in all
- stretch_order: int32 [32], replicated, may hold values from 0 to 31, as said below
Outputs:
- draft_grad: float32 [2048, 2048], P('ctx', 'vocab')
Inputs may be any that keep to these rules, and one draw needn't show every extreme that they name: `rollout_lengths`: the lengths add up to 2048. `stretch_order`: each block number appears once; entries 2c and 2c + 1 add up to 31.
All inputs are finite; a program needn't handle non-finite values.
Results may differ from a plain program's by a relative error of at most 0.0045.
Values may be sent and summed in bfloat16 or wider, within the bound.
No kernel may reach another device: no remote copies, remote signals or barrier semaphores. Data moves between devices by JAX's collectives and lax.ppermute only.
A program may use at most 128 MiB of HBM per device.

v0:
```python
import jax
import jax.numpy as jnp
from jax import lax
from jax.experimental import pallas as pl
from jax.experimental.pallas import tpu as pltpu
from jax.sharding import Mesh
from jax.sharding import PartitionSpec as P


HEAD_DIM = 128
EPSILON = 1e-05
ROPE_BASE = 500000.0
MIXING = 0.5
NEGATIVE = -1e30

CTX = ("yh", "z", "c")
VOCAB = ("x", "yl")
X, Y, Z, C = ("x",), ("yh", "yl"), ("z",), ("c",)
CHIPS = ("yh", "z", "x", "yl")
F32, BF16 = jnp.float32, jnp.bfloat16


def shifted(a, axes, k):
    n = lax.axis_size(axes)
    return lax.ppermute(a, axes, [(i, (i + k) % n) for i in range(n)])


def ring(a, axes):
    n = lax.axis_size(axes)
    return [a] + [shifted(a, axes, n - d) for d in range(1, n)]


def rms_scale(values, gain):
    mean_square = jnp.mean(values * values, axis=-1, keepdims=True)
    return values * lax.rsqrt(mean_square + EPSILON) * gain


def rotate(vectors, positions):
    half_dim = vectors.shape[-1] // 2
    exponents = jnp.arange(half_dim, dtype=F32) * (2.0 / vectors.shape[-1])
    frequencies = jnp.power(ROPE_BASE, -exponents)
    angles = positions.astype(F32)[:, None] * frequencies[None, :]
    cosine_values = jnp.cos(angles)[:, None, :]
    sine_values = jnp.sin(angles)[:, None, :]
    leading = vectors[..., :half_dim]
    trailing = vectors[..., half_dim:]
    return jnp.concatenate(
        [
            leading * cosine_values - trailing * sine_values,
            trailing * cosine_values + leading * sine_values,
        ],
        axis=-1,
    )


NT = (((1,), (1,)), ((), ()))


BLOCK = 256


def fetch_words(own_ref, other_ref, held_ref, arrived):
    j, steps = pl.program_id(0), pl.num_programs(0)
    half = steps // 2

    def start(step, slot):
        @pl.when(step < half)
        def _():
            at = pl.ds(pl.multiple_of(step * BLOCK, BLOCK), BLOCK)
            pltpu.make_async_copy(own_ref.at[at], held_ref.at[slot], arrived.at[slot]).start()

        @pl.when(step >= half)
        def _():
            at = pl.ds(pl.multiple_of((step - half) * BLOCK, BLOCK), BLOCK)
            pltpu.make_async_copy(other_ref.at[at], held_ref.at[slot], arrived.at[slot]).start()

    @pl.when(j == 0)
    def _():
        start(0, 0)

    @pl.when(j + 1 < steps)
    def _():
        start(j + 1, (j + 1) % 2)

    slot = j % 2
    pltpu.make_async_copy(own_ref.at[pl.ds(0, BLOCK)], held_ref.at[slot], arrived.at[slot]).wait()
    return slot


def logits_step(slot, x_ref, held_ref, out_ref, top_ref, sum_ref):
    @pl.when(pl.program_id(0) == 0)
    def _():
        top_ref[...] = jnp.full_like(top_ref, NEGATIVE)
        sum_ref[...] = jnp.zeros_like(sum_ref)

    part = lax.dot_general(x_ref[...], held_ref[slot], NT, preferred_element_type=F32)
    out_ref[...] = part
    pieces = [part[:, k : k + 128] for k in range(0, BLOCK, 128)]
    old = top_ref[...]
    new = old
    for piece in pieces:
        new = jnp.maximum(new, piece)
    total = sum_ref[...] * jnp.exp(old - new)
    for piece in pieces:
        total = total + jnp.exp(piece - new)
    sum_ref[...] = total
    top_ref[...] = new


def totals_rows(top_ref, sum_ref):
    shape = top_ref.shape
    lanes = top_ref[...]
    top = jnp.max(lanes, axis=1, keepdims=True)
    total = jnp.sum(sum_ref[...] * jnp.exp(lanes - top), axis=1, keepdims=True)
    lane = lax.broadcasted_iota(jnp.int32, shape, 1)
    both = jnp.where(lane == 0, jnp.broadcast_to(top, shape), jnp.broadcast_to(total, shape))
    return jnp.transpose(both)


HELD = pl.BlockSpec(memory_space=pltpu.HBM)


def logits_scratch(count, width):
    return [
        pltpu.VMEM((count, width), BF16),
        pltpu.VMEM((2, BLOCK, width), BF16),
        pltpu.SemaphoreType.DMA((2,)),
        pltpu.VMEM((count, 128), F32),
        pltpu.VMEM((count, 128), F32),
    ]


def draft_kernel(place, *refs):
    near_ref, ahead_ref, behind_ref = refs[0:3]
    own_ref, other_ref, out_ref, stats_ref, x_ref, held_ref, arrived, top_ref, sum_ref = refs[5:]
    slot = fetch_words(own_ref, other_ref, held_ref, arrived)

    @pl.when(pl.program_id(0) == 0)
    def _():
        for dz in range(4):
            pz = (place[2] + dz) % 4
            for dyh in range(2):
                base = (place[1] // 2 + dyh) % 2 * 128 + pz * 32
                for x in range(4):
                    at = pl.ds(pl.multiple_of(base + x * 256, 32), 32)
                    if dz == 2:
                        x_ref[at, :] = refs[3 + dyh][x]
                    else:
                        x_ref[at, :] = (near_ref, ahead_ref, None, behind_ref)[dz][dyh, x]

    logits_step(slot, x_ref, held_ref, out_ref, top_ref, sum_ref)

    @pl.when(pl.program_id(0) == pl.num_programs(0) - 1)
    def _():
        stats_ref[...] = totals_rows(top_ref, sum_ref)[:8]


def draft_logits(place, rows, own, other):
    words, width = 2 * own.shape[0], own.shape[1]
    count = 1024
    return pl.pallas_call(
        draft_kernel,
        grid_spec=pltpu.PrefetchScalarGridSpec(
            num_scalar_prefetch=1,
            grid=(words // BLOCK,),
            in_specs=[
                pl.BlockSpec(r.shape, lambda j, s, n=r.ndim: (0,) * n, pipeline_mode=pl.Buffered(1))
                for r in rows
            ]
            + [HELD, HELD],
            out_specs=[
                pl.BlockSpec((count, BLOCK), lambda j, s: (0, j)),
                pl.BlockSpec((8, count), lambda j, s: (0, 0)),
            ],
            scratch_shapes=logits_scratch(count, width),
        ),
        out_shape=[
            jax.ShapeDtypeStruct((count, words), F32),
            jax.ShapeDtypeStruct((8, count), F32),
        ],
        compiler_params=pltpu.CompilerParams(vmem_limit_bytes=40 << 20),
        cost_estimate=pl.CostEstimate(
            flops=2 * count * words * width, transcendentals=count * words, bytes_accessed=12 << 20
        ),
        name="draft_logits",
    )(place, *rows, own, other)


def teacher_kernel(place, *refs):
    a_refs, b_refs, c_refs = refs[0:4], refs[4:8], refs[8:12]
    own_ref, other_ref, draft_stats, out_ref, stats_ref = refs[12:17]
    x_ref, held_ref, arrived, top_ref, sum_ref = refs[17:]
    slot = fetch_words(own_ref, other_ref, held_ref, arrived)

    @pl.when(pl.program_id(0) == 0)
    def _():
        a_width, b_width = a_refs[0].shape[-1], b_refs[0].shape[-1]
        for dx in range(4):
            px = (place[0] + dx) % 4
            for dy in range(4):
                py = (place[1] + dy) % 4
                for dz in range(4):
                    pz = (place[2] + dz) % 4
                    row = px * 256 + (py // 2) * 128 + pz * 32 + (py % 2) * 16
                    at = pl.ds(pl.multiple_of(row, 16), 16)
                    x_ref[at, :a_width] = a_refs[dx][dy, dz]
                    x_ref[at, a_width : a_width + b_width] = b_refs[dy][dz, dx]
                    x_ref[at, a_width + b_width :] = c_refs[dz][dx, dy]

    logits_step(slot, x_ref, held_ref, out_ref, top_ref, sum_ref)

    @pl.when(pl.program_id(0) == pl.num_programs(0) - 1)
    def _():
        teacher = totals_rows(top_ref, sum_ref)
        stats_ref[...] = jnp.concatenate([teacher[0:2], draft_stats[0:2], teacher[4:8]], axis=0)


def teacher_logits(place, parts, own, other, draft_stats):
    words, width = 2 * own.shape[0], own.shape[1]
    count = 1024
    whole = [
        pl.BlockSpec(p.shape, lambda j, s: (0, 0, 0, 0), pipeline_mode=pl.Buffered(1))
        for p in parts
    ]
    return pl.pallas_call(
        teacher_kernel,
        grid_spec=pltpu.PrefetchScalarGridSpec(
            num_scalar_prefetch=1,
            grid=(words // BLOCK,),
            in_specs=whole + [HELD, HELD, pl.BlockSpec((8, count), lambda j, s: (0, 0))],
            out_specs=[
                pl.BlockSpec((count, BLOCK), lambda j, s: (0, j)),
                pl.BlockSpec((8, count), lambda j, s: (0, 0)),
            ],
            scratch_shapes=logits_scratch(count, width),
        ),
        out_shape=[
            jax.ShapeDtypeStruct((count, words), F32),
            jax.ShapeDtypeStruct((8, count), F32),
        ],
        compiler_params=pltpu.CompilerParams(vmem_limit_bytes=48 << 20),
        cost_estimate=pl.CostEstimate(
            flops=2 * count * words * width, transcendentals=count * words, bytes_accessed=20 << 20
        ),
        name="teacher_logits",
    )(place, *parts, own, other, draft_stats)


def gradient_kernel(starts, teacher_ref, draft_ref, rows_ref, own_ref, other_ref, out_ref, delta_ref):
    count, words = teacher_ref.shape
    column = jnp.transpose(jnp.concatenate([rows_ref[...]] * 16, axis=0))
    half = words // 2
    lane = lax.broadcasted_iota(jnp.int32, (count, half), 1)
    wanted = column[:, 4:5].astype(jnp.int32)
    for h in range(2):
        at = slice(h * half, (h + 1) * half)
        teacher = jnp.exp(teacher_ref[:, at] - column[:, 0:1]) * column[:, 1:2]
        draft = jnp.exp(draft_ref[:, at] - column[:, 2:3]) * column[:, 3:4]
        soft = teacher + jnp.where(lane + starts[h] == wanted, MIXING, 0.0)
        delta_ref[:, at] = (draft - soft).astype(BF16)
    total = jnp.dot(delta_ref[:, :half], own_ref[...], preferred_element_type=F32)
    total = total + jnp.dot(delta_ref[:, half:], other_ref[...], preferred_element_type=F32)
    total = total.astype(BF16)
    for f in range(8):
        for t in range(8):
            out_ref[t, f, 0] = total[t * 32 : t * 32 + 32, f * 256 : f * 256 + 256]


def gradient_parts(starts, teacher, draft, rows, own, other):
    count, words = teacher.shape
    width = own.shape[1]
    tile = 256
    held = pl.BlockSpec(own.shape, lambda j, s: (0, 0), pipeline_mode=pl.Buffered(1))
    return pl.pallas_call(
        gradient_kernel,
        grid_spec=pltpu.PrefetchScalarGridSpec(
            num_scalar_prefetch=1,
            grid=(count // tile,),
            in_specs=[
                pl.BlockSpec((tile, words), lambda j, s: (j, 0)),
                pl.BlockSpec((tile, words), lambda j, s: (j, 0)),
                pl.BlockSpec((8, tile), lambda j, s: (0, j)),
                held,
                held,
            ],
            out_specs=pl.BlockSpec((8, 8, 1, 32, 256), lambda j, s: (0, 0, j, 0, 0)),
            scratch_shapes=[pltpu.VMEM((tile, words), BF16)],
        ),
        out_shape=jax.ShapeDtypeStruct((8, 8, 4, 32, 256), BF16),
        compiler_params=pltpu.CompilerParams(vmem_limit_bytes=40 << 20),
        cost_estimate=pl.CostEstimate(
            flops=2 * count * words * width, transcendentals=2 * count * words, bytes_accessed=16 << 20
        ),
        name="gradient_parts",
    )(starts, teacher, draft, rows, own, other)


def on_device(
    hidden_in,
    attn_gain,
    w_query,
    w_key,
    w_value,
    w_out,
    final_gain,
    teacher_head,
    draft_rows,
    draft_head,
    target_ids,
    rollout_lengths,
    stretch_order,
):
    row_count = hidden_in.shape[0]
    head_dim = HEAD_DIM
    local_heads = w_query.shape[1] // head_dim
    local_groups = w_key.shape[1] // head_dim
    group_size = local_heads // local_groups
    half_rows = row_count // 2
    stretch_ids = jnp.arange(stretch_order.shape[0], dtype=jnp.int32)
    rollout_ends = jnp.cumsum(rollout_lengths)
    my_x, my_yh, my_yl = lax.axis_index("x"), lax.axis_index("yh"), lax.axis_index("yl")
    my_z, my_c = lax.axis_index("z"), lax.axis_index("c")

    def locate(row_ids):
        stretch_hit = (row_ids // half_rows)[:, None] == stretch_ids[None, :]
        stretch_start = jnp.sum(jnp.where(stretch_hit, stretch_order[None, :], 0), axis=1)
        positions = stretch_start * half_rows + row_ids % half_rows
        rollouts = jnp.sum((positions[:, None] >= rollout_ends[None, :]).astype(jnp.int32), axis=1)
        return (positions, rollouts)

    lines = jnp.arange(row_count, dtype=jnp.int32)
    query_pos, query_roll = locate(lax.axis_index(CTX) * row_count + lines)
    normed = rms_scale(hidden_in.astype(F32), attn_gain).astype(BF16)
    keys = jnp.dot(normed, w_key, preferred_element_type=F32).reshape(
        row_count, local_groups, head_dim
    )
    keys = rotate(keys, query_pos).astype(BF16).reshape(row_count, local_groups * head_dim)
    values = jnp.dot(normed, w_value, preferred_element_type=F32).astype(BF16)
    both = jnp.concatenate([keys, values], axis=1)
    copies = jnp.broadcast_to(both[None], (8, *both.shape))
    both = lax.all_to_all(copies, ("yh", "z"), split_axis=0, concat_axis=0, tiled=True)
    gathered = both
    both = both.reshape(8 * row_count, -1)
    both = jnp.concatenate(ring(both, C), axis=0)
    key_width = local_groups * head_dim
    key_piece = both[:, :key_width].reshape(-1, local_groups, head_dim)
    value_piece = both[:, key_width:].reshape(-1, local_groups, head_dim)

    queries = jnp.dot(normed, w_query, preferred_element_type=F32).reshape(
        row_count, local_heads, head_dim
    )
    queries = (
        rotate(queries, query_pos)
        .astype(BF16)
        .reshape(row_count, local_groups, group_size, head_dim)
    )
    slots = jnp.arange(key_piece.shape[0], dtype=jnp.int32)
    slot = slots // row_count
    from_c = (my_c + slot // 8) % 2
    owner = slot % 8 * 2 + from_c
    key_pos, key_roll = locate(owner * row_count + slots % row_count)
    allowed = (key_pos[None, :] <= query_pos[:, None]) & (key_roll[None, :] == query_roll[:, None])
    visible = allowed[:, None, None, :]
    scores = jnp.einsum(
        "tkgd,nkd->tkgn", queries, key_piece, preferred_element_type=F32
    ) * head_dim ** (-0.5)
    scores = jnp.where(visible, scores, NEGATIVE)
    top = jnp.max(scores, axis=-1)
    weights = jnp.where(visible, jnp.exp(scores - top[..., None]), 0.0)
    weight_sum = jnp.sum(weights, axis=-1)
    weighted = jnp.einsum(
        "tkgn,nkd->tkgd", weights.astype(BF16), value_piece, preferred_element_type=F32
    )
    attended = (
        (weighted / weight_sum[..., None]).astype(BF16).reshape(row_count, local_heads * head_dim)
    )

    partial_value = jnp.dot(attended, w_out, preferred_element_type=F32).astype(BF16)
    shares = lax.axis_size(VOCAB)
    share_rows = row_count // shares
    arrived = lax.all_to_all(
        partial_value.reshape(shares, share_rows, -1),
        VOCAB,
        split_axis=0,
        concat_axis=0,
        tiled=True,
    )
    own_rows = lax.dynamic_slice_in_dim(
        hidden_in, lax.axis_index(VOCAB) * share_rows, share_rows, 0
    )
    mixed = own_rows.astype(F32) + jnp.sum(arrived.astype(F32), axis=0)
    final = rms_scale(mixed, final_gain).astype(BF16)

    teacher_other = shifted(teacher_head, C, 1)
    draft_other = shifted(draft_head, C, 1)

    place = jnp.stack([my_x, my_yh * 2 + my_yl, my_z]).astype(jnp.int32)
    near = jnp.stack(ring(draft_rows, ("yh",)))
    near, _ = lax.optimization_barrier((near, gathered))
    near = near.reshape(2, 4, 2 * share_rows, -1)
    ahead, behind = shifted(near, Z, 3), shifted(near, Z, 1)
    far = [shifted(ahead[0], Z, 3), shifted(behind[1], Z, 1)]
    draft_part, draft_stats = draft_logits(
        place, [near, ahead, behind] + far, draft_head, draft_other
    )

    a, b, c = jnp.split(final, [1408, 2816], axis=1)
    a, b, c = ring(a, Z), ring(b, X), ring(c, Y)
    a, b, c = jnp.stack(a), jnp.stack(b), jnp.stack(c)
    a = jnp.stack(ring(a, Y))
    b = jnp.stack(ring(b, Z))
    c = jnp.stack(ring(c, X))
    a, b, c = ring(a, X), ring(b, Y), ring(c, Z)
    teacher_part, stats = teacher_logits(
        place, a + b + c, teacher_head, teacher_other, draft_stats
    )

    for axes in (("x", "yl"), ("yh", "z")):
        copies = jnp.broadcast_to(stats[None, :4], (8, *stats[:4].shape))
        pieces = lax.all_to_all(copies, axes, split_axis=0, concat_axis=0, tiled=True)
        tops = jnp.max(pieces[:, 0::2], axis=0)
        sums = jnp.sum(pieces[:, 1::2] * jnp.exp(pieces[:, 0::2] - tops), axis=0)
        stats = jnp.stack([tops[0], sums[0], tops[1], sums[1]])
    targets = target_ids.reshape(2, 4, 2, 4, 2 * share_rows)
    targets = lax.dynamic_index_in_dim(targets, my_c, 2, keepdims=False)
    targets = jnp.transpose(targets, (2, 0, 1, 3)).reshape(-1).astype(F32)
    nothing = jnp.zeros_like(targets)
    rows = jnp.stack(
        [
            stats[0],
            (1.0 - MIXING) / stats[1],
            stats[2],
            1.0 / stats[3],
            targets,
            nothing,
            nothing,
            nothing,
        ]
    )
    word_count = teacher_head.shape[0]
    block_id = lax.axis_index(VOCAB) * lax.axis_size(CTX) + (my_yh * 4 + my_z) * 2
    starts = jnp.stack([block_id + my_c, block_id + 1 - my_c]).astype(jnp.int32) * word_count
    parts = gradient_parts(starts, teacher_part, draft_part, rows, draft_head, draft_other)
    parts = parts.reshape(64, row_count, -1)
    arrived = lax.all_to_all(parts, CHIPS, split_axis=0, concat_axis=0, tiled=True)
    return jnp.sum(arrived.astype(F32), axis=0)


def solution(mesh):
    torus = Mesh(mesh.devices.reshape(2, 4, 2, 4, 2), ("yh", "z", "c", "x", "yl"))
    words = P(("x", "yl", "yh", "z", "c"), None)

    return jax.shard_map(
        on_device,
        mesh=torus,
        in_specs=(
            P(CTX, None),
            P(),
            P(None, VOCAB),
            P(None, VOCAB),
            P(None, VOCAB),
            P(VOCAB, None),
            P(),
            words,
            P(CTX, None),
            words,
            P(),
            P(),
            P(),
        ),
        out_specs=P(CTX, VOCAB),
        check_vma=False,
    )
```

profile of v0, /device:TPU:0, one launch (start us, length us, event | category | flops | bytes accessed | tf_op | source)
XLA Modules:
  0.0 318.8 jit_solution(1234169608380142213)
XLA Ops:
  1.0 1.5 fusion.3
  2.5 1.8 convolution_convert_fusion.1
  4.3 2.2 convolution_bitcast_fusion
  7.7 8.2 %all-to-all-start = ((bf16[8,128,256]{2,1,0:T(8,128)(2,1)}), bf16[8,128,256]{2,1,0:T(8,128)(2,1)S(1)}, u32[]{:S(2)}, u32[]{:S(2)}) async-start(bf16[8,128,256]{2,1,0:T(8,128)(2,1)} %broadcast_in_dim.46), calls=%async_computation | async-start | bytes 1048576 | tf_op jit(solution)/shard_map/all_to_all | solution.py:341
  16.1 2.9 fusion.69
  20.0 6.9 %all-to-all-done = bf16[8,128,256]{2,1,0:T(8,128)(2,1)S(1)} async-done(((bf16[8,128,256]{2,1,0:T(8,128)(2,1)}), bf16[8,128,256]{2,1,0:T(8,128)(2,1)S(1)}, u32[]{:S(2)}, u32[]{:S(2)}) %all-to-all-start) | async-done | bytes 524320 | tf_op jit(solution)/shard_map/all_to_all | solution.py:341
  27.0 1.3 compare_and_fusion
  29.7 1.0 fusion.1
  30.7 1.1 fusion.16
  31.9 1.0 copy-done.21
  32.9 1.8 convolution_convert_fusion
  34.7 4.6 %all-to-all-start.1 = ((bf16[8,16,4096]{2,1,0:T(8,128)(2,1)}), bf16[8,16,4096]{2,1,0:T(8,128)(2,1)}, u32[]{:S(2)}, u32[]{:S(2)}) async-start(bf16[8,16,4096]{2,1,0:T(8,128)(2,1)} %bitcast.19), calls=%async_computation.1 | async-start | bytes 2097152 | tf_op jit(solution)/shard_map/all_to_all | solution.py:381
  39.3 1.8 collective-permute-start.29
  41.6 22.8 %collective-permute-done.29 = bf16[128,2048]{1,0:T(8,128)(2,1)S(1)} collective-permute-done((bf16[128,2048]{1,0:T(8,128)(2,1)S(1)}, bf16[128,2048]{1,0:T(8,128)(2,1)S(1)}, u32[]{:S(2)}, u32[]{:S(2)}) %collective-permute-start.29) | collective-permute-done | bytes 524320 | tf_op jit(solution)/shard_map/ppermute | solution.py:25
  65.1 1.3 pad_maximum_fusion
  66.4 1.5 collective-permute-start.30
  68.5 1.4 convert_reduce_fusion.1
  69.9 1.1 multiply_reduce_fusion
  71.0 1.0 multiply_convert_fusion
  72.0 1.2 collective-permute-start.21
  73.2 17.7 %collective-permute-done.30.refs_1_ = bf16[2,4,32,2048]{3,2,1,0:T(8,128)(2,1)} collective-permute-done((bf16[2,4,32,2048]{3,2,1,0:T(8,128)(2,1)S(1)}, bf16[2,4,32,2048]{3,2,1,0:T(8,128)(2,1)}, u32[]{:S(2)}, u32[]{:S(2)}) %collective-permute-start.30) | collective-permute-done | bytes 1048608 | tf_op jit(solution)/shard_map/ppermute | solution.py:25
  91.0 2.0 collective-permute-start.20
  93.4 2.1 collective-permute-start.19
  96.5 2.3 collective-permute-start.2
  98.7 1.3 collective-permute-start.1
  100.8 1.7 collective-permute-start.12
  102.5 3.5 %collective-permute-start.11 = (bf16[16,1408]{1,0:T(8,128)(2,1)S(1)}, bf16[16,1408]{1,0:T(8,128)(2,1)S(1)}, u32[]{:S(2)}, u32[]{:S(2)}) collective-permute-start(bf16[16,1408]{1,0:T(8,128)(2,1)S(1)} %get-tuple-element.31), channel_id=1, source_target_pairs={{0,4},{2,6},{4,0},{6,2},{1,5},{3,7},{5,1},{7,3},{8,12},{10,14},{12... | collective-permute-start | bytes 135176 | tf_op jit(solution)/shard_map/ppermute | solution.py:25
  106.3 1.1 slice_bitcast_fusion.1
  107.4 2.7 collective-permute-start.32
  110.1 2.1 collective-permute-start.23
  112.2 1.7 collective-permute-done.24
  114.3 1.1 slice_bitcast_fusion
  115.4 1.5 collective-permute-done.23
  116.9 2.5 collective-permute-done.22
  119.5 2.7 collective-permute-start.10
  122.2 1.6 collective-permute-done.10
  123.8 1.4 collective-permute-start.25
  126.3 2.2 collective-permute-done.33.refs_4_
  128.4 1.8 collective-permute-start.5
  130.2 1.7 collective-permute-start.4
  132.7 2.7 collective-permute-done.5
  135.4 1.6 collective-permute-done.4
  138.8 3.5 %collective-permute-start.7 = (bf16[4,4,16,1408]{3,2,1,0:T(8,128)(2,1)}, bf16[4,4,16,1408]{3,2,1,0:T(8,128)(2,1)S(1)}, u32[]{:S(2)}, u32[]{:S(2)}) collective-permute-start(bf16[4,4,16,1408]{3,2,1,0:T(8,128)(2,1)} %pad_maximum_fusion.1.refs_0_), channel_id=1, source_target_pairs={{0,6},{2,0},{4,2},{6,4},{1,7},{3,1},{5,3},{7,5},{8,14},{10,8},{12,... | collective-permute-start | bytes 2162696 | tf_op jit(solution)/shard_map/ppermute | solution.py:25
  142.4 1.5 collective-permute-start.8
  143.9 2.2 collective-permute-start.26
  146.2 2.1 collective-permute-start.27
  149.2 13.8 %collective-permute-done.26.refs_10_ = bf16[4,4,16,1280]{3,2,1,0:T(8,128)(2,1)S(1)} collective-permute-done((bf16[4,4,16,1280]{3,2,1,0:T(8,128)(2,1)S(1)}, bf16[4,4,16,1280]{3,2,1,0:T(8,128)(2,1)S(1)}, u32[]{:S(2)}, u32[]{:S(2)}) %collective-permute-start.26) | collective-permute-done | bytes 655392 | tf_op jit(solution)/shard_map/ppermute | solution.py:25
  164.8 6.3 %collective-permute-done.27.refs_11_ = bf16[4,4,16,1280]{3,2,1,0:T(8,128)(2,1)S(1)} collective-permute-done((bf16[4,4,16,1280]{3,2,1,0:T(8,128)(2,1)S(1)}, bf16[4,4,16,1280]{3,2,1,0:T(8,128)(2,1)S(1)}, u32[]{:S(2)}, u32[]{:S(2)}) %collective-permute-start.27) | collective-permute-done | bytes 655392 | tf_op jit(solution)/shard_map/ppermute | solution.py:25
  172.0 2.5 collective-permute-start.16
  177.2 1.0 copy-done.18
  178.2 1.0 copy-done.20
  179.3 9.1 %draft_logits.1 = (f32[1024,1024]{1,0:T(8,128)S(1)}, f32[8,1024]{1,0:T(8,128)S(1)}) custom-call(s32[3]{0:T(128)S(1)} %pad_add_fusion.place, bf16[2,4,32,2048]{3,2,1,0:T(8,128)(2,1)S(1)} %bitcast.112, bf16[2,4,32,2048]{3,2,1,0:T(8,128)(2,1)} %collective-permute-done.30.refs_1_, bf16[2,4,32,2048]{3,2,1,0:T(8,128)(2,1)} %collective-permute-done.31.refs_2_, ...), custom_call_target="tpu_custom_call" | custom-call | flops 4294967296 | bytes 12582912 | tf_op jit(solution)/shard_map/draft_logits/pallas_call | solution.py:161
  188.4 2.0 copy-done.2
  190.4 15.5 %collective-permute-done.16.refs_5_ = bf16[4,4,16,1408]{3,2,1,0:T(8,128)(2,1)} collective-permute-done((bf16[4,4,16,1408]{3,2,1,0:T(8,128)(2,1)}, bf16[4,4,16,1408]{3,2,1,0:T(8,128)(2,1)}, u32[]{:S(2)}, u32[]{:S(2)}) %collective-permute-start.16) | collective-permute-done | bytes 720928 | tf_op jit(solution)/shard_map/ppermute | solution.py:25
  206.0 4.6 %collective-permute-done.18.refs_7_ = bf16[4,4,16,1408]{3,2,1,0:T(8,128)(2,1)} collective-permute-done((bf16[4,4,16,1408]{3,2,1,0:T(8,128)(2,1)}, bf16[4,4,16,1408]{3,2,1,0:T(8,128)(2,1)}, u32[]{:S(2)}, u32[]{:S(2)}) %collective-permute-start.18) | collective-permute-done | bytes 720928 | tf_op jit(solution)/shard_map/ppermute | solution.py:25
  210.6 16.3 %teacher_logits.1 = (f32[1024,1024]{1,0:T(8,128)}, f32[8,1024]{1,0:T(8,128)S(1)}) custom-call(s32[3]{0:T(128)S(1)} %pad_add_fusion.place, bf16[4,4,16,1408]{3,2,1,0:T(8,128)(2,1)} %pad_maximum_fusion.1.refs_0_, bf16[4,4,16,1408]{3,2,1,0:T(8,128)(2,1)S(1)} %copy-done.8, bf16[4,4,16,1408]{3,2,1,0:T(8,128)(2,1)S(1)} %copy-done.10, ...), custom_call_target="tpu_custom_call" | custom-call | flops 8589934592 | bytes 20971520 | tf_op jit(solution)/shard_map/teacher_logits/pallas_call | solution.py:225
  227.6 3.4 %all-to-all-start.2 = ((f32[8,4,1024]{2,1,0:T(4,128)}), f32[8,4,1024]{2,1,0:T(4,128)S(1)}, u32[]{:S(2)}, u32[]{:S(2)}) async-start(f32[8,4,1024]{2,1,0:T(4,128)} %broadcast_in_dim.56), calls=%async_computation.2 | async-start | bytes 262144 | tf_op jit(solution)/shard_map/all_to_all | solution.py:420
  231.1 6.3 %all-to-all-done.2 = f32[8,4,1024]{2,1,0:T(4,128)S(1)} async-done(((f32[8,4,1024]{2,1,0:T(4,128)}), f32[8,4,1024]{2,1,0:T(4,128)S(1)}, u32[]{:S(2)}, u32[]{:S(2)}) %all-to-all-start.2) | async-done | bytes 131104 | tf_op jit(solution)/shard_map/all_to_all | solution.py:420
  238.5 4.5 %all-to-all-start.3 = ((f32[8,4,1024]{2,1,0:T(4,128)}), f32[8,4,1024]{2,1,0:T(4,128)S(1)}, u32[]{:S(2)}, u32[]{:S(2)}) async-start(f32[8,4,1024]{2,1,0:T(4,128)} %broadcast_in_dim.57), calls=%async_computation.3 | async-start | bytes 262144 | tf_op jit(solution)/shard_map/all_to_all | solution.py:420
  243.2 7.9 %all-to-all-done.3 = f32[8,4,1024]{2,1,0:T(4,128)S(1)} async-done(((f32[8,4,1024]{2,1,0:T(4,128)}), f32[8,4,1024]{2,1,0:T(4,128)S(1)}, u32[]{:S(2)}, u32[]{:S(2)}) %all-to-all-start.3) | async-done | bytes 131104 | tf_op jit(solution)/shard_map/all_to_all | solution.py:420
  251.6 2.2 copy-done.3
  253.8 9.5 %gradient_parts.1 = bf16[8,8,4,32,256]{4,3,2,1,0:T(8,128)(2,1)S(1)} custom-call(s32[2]{0:T(128)S(1)} %add_multiply_fusion.starts, f32[1024,1024]{1,0:T(8,128)S(1)} %copy-done.3, f32[1024,1024]{1,0:T(8,128)} %copy-done.2, f32[8,1024]{1,0:T(8,128)S(1)} %stack.174.rows_ref, bf16[512,2048]{1,0:T(8,128)(2,1)S(1)} %copy-done.4, ...), custom_call_target="tpu_custom_call" | custom-call | flops 4294967296 | bytes 16777216 | tf_op jit(solution)/shard_map/gradient_parts/pallas_call | solution.py:274
  263.3 54.2 %all_to_all.25 = bf16[64,128,256]{2,1,0:T(8,128)(2,1)S(1)} all-to-all(bf16[64,128,256]{2,1,0:T(8,128)(2,1)S(1)} %bitcast.109), channel_id=1, replica_groups=mesh['yh'=2,'z'=4,'c'=2,'x'=4,'yl'=2] {'yh','z','x','yl'}, dimensions={0} | all-to-all | bytes 8388608 | tf_op jit(solution)/shard_map/all_to_all | solution.py:445
  317.5 1.2 convert_reduce_fusion
  (146 shorter events, 22.0 us)
Async XLA Ops:
  0.0 2.5 copy-start
  0.0 15.9 %copy-start.27 = (s32[32]{0:T(128)S(1)}, s32[32]{0:T(128)}, u32[]{:S(2)}) copy-start(s32[32]{0:T(128)} %param.25) | copy-start | bytes 388
  0.0 16.1 %copy-start.22 = (bf16[128,4096]{1,0:T(8,128)(2,1)S(1)}, bf16[128,4096]{1,0:T(8,128)(2,1)}, u32[]{:S(2)}) copy-start(bf16[128,4096]{1,0:T(8,128)(2,1)} %param.13) | copy-start | bytes 3145732
  0.0 16.1 %copy-start.28 = (f32[4096]{0:T(1024)S(1)}, f32[4096]{0:T(1024)}, u32[]{:S(2)}) copy-start(f32[4096]{0:T(1024)} %param.14) | copy-start | bytes 49156
  7.7 11.7 %copy-start.29 = (s32[4]{0:T(128)S(1)}, s32[4]{0:T(128)}, u32[]{:S(2)}) copy-start(s32[4]{0:T(128)} %param.24) | copy-start | bytes 52
  7.7 19.2 %all-to-all-start = ((bf16[8,128,256]{2,1,0:T(8,128)(2,1)}), bf16[8,128,256]{2,1,0:T(8,128)(2,1)S(1)}, u32[]{:S(2)}, u32[]{:S(2)}) async-start(bf16[8,128,256]{2,1,0:T(8,128)(2,1)} %broadcast_in_dim.46), calls=%async_computation | async-start | bytes 1048576 | tf_op jit(solution)/shard_map/all_to_all | solution.py:341
  26.9 1.9 collective-permute-start
  30.7 2.2 copy-start.21
  31.9 7.4 %copy-start.23 = (bf16[128,2048]{1,0:T(8,128)(2,1)S(1)}, bf16[128,2048]{1,0:T(8,128)(2,1)}, u32[]{:S(2)}) copy-start(bf16[128,2048]{1,0:T(8,128)(2,1)} %param.21) | copy-start | bytes 1572868
  31.9 9.2 %copy-start.4 = (bf16[512,2048]{1,0:T(8,128)(2,1)S(1)}, bf16[512,2048]{1,0:T(8,128)(2,1)}, u32[]{:S(2)}) copy-start(bf16[512,2048]{1,0:T(8,128)(2,1)} %own_ref.1) | copy-start | bytes 6291460
  34.7 36.3 %copy-start.25 = (f32[4096]{0:T(1024)S(1)}, f32[4096]{0:T(1024)}, u32[]{:S(2)}) copy-start(f32[4096]{0:T(1024)} %param.19) | copy-start | bytes 49156
  34.7 33.8 %all-to-all-start.1 = ((bf16[8,16,4096]{2,1,0:T(8,128)(2,1)}), bf16[8,16,4096]{2,1,0:T(8,128)(2,1)}, u32[]{:S(2)}, u32[]{:S(2)}) async-start(bf16[8,16,4096]{2,1,0:T(8,128)(2,1)} %bitcast.19), calls=%async_computation.1 | async-start | bytes 2097152 | tf_op jit(solution)/shard_map/all_to_all | solution.py:381
  39.3 25.1 %collective-permute-start.29 = (bf16[128,2048]{1,0:T(8,128)(2,1)S(1)}, bf16[128,2048]{1,0:T(8,128)(2,1)S(1)}, u32[]{:S(2)}, u32[]{:S(2)}) collective-permute-start(bf16[128,2048]{1,0:T(8,128)(2,1)S(1)} %copy-done.23), channel_id=1, source_target_pairs={{0,64},{64,0},{1,65},{65,1},{2,66},{66,2},{3,67},{67,3},{4,68},{68... | collective-permute-start | bytes 1572872 | tf_op jit(solution)/shard_map/ppermute | solution.py:25
  41.0 169.5 %collective-permute-start.28 = (bf16[512,4096]{1,0:T(8,128)(2,1)}, bf16[512,4096]{1,0:T(8,128)(2,1)}, u32[]{:S(2)}, u32[]{:S(2)}) collective-permute-start(bf16[512,4096]{1,0:T(8,128)(2,1)} %refs_12_.1), channel_id=1, source_target_pairs={{0,8},{8,0},{1,9},{9,1},{2,10},{10,2},{3,11},{11,3},{4,12},{12,4},... | collective-permute-start | bytes 12582920 | tf_op jit(solution)/shard_map/ppermute | solution.py:25
  41.0 89.2 %collective-permute-start.34 = (bf16[512,2048]{1,0:T(8,128)(2,1)S(1)}, bf16[512,2048]{1,0:T(8,128)(2,1)}, u32[]{:S(2)}, u32[]{:S(2)}) collective-permute-start(bf16[512,2048]{1,0:T(8,128)(2,1)S(1)} %copy-done.4), channel_id=1, source_target_pairs={{0,8},{8,0},{1,9},{9,1},{2,10},{10,2},{3,11},{11,3},{4,12},{12,4},... | collective-permute-start | bytes 6291464 | tf_op jit(solution)/shard_map/ppermute | solution.py:25
  66.4 24.5 %collective-permute-start.30 = (bf16[2,4,32,2048]{3,2,1,0:T(8,128)(2,1)S(1)}, bf16[2,4,32,2048]{3,2,1,0:T(8,128)(2,1)}, u32[]{:S(2)}, u32[]{:S(2)}) collective-permute-start(bf16[2,4,32,2048]{3,2,1,0:T(8,128)(2,1)S(1)} %bitcast.110), channel_id=1, source_target_pairs={{0,48},{16,0},{32,16},{48,32},{1,49},{17,1},{33,17},{49,33},{2,50}... | collective-permute-start | bytes 3145736 | tf_op jit(solution)/shard_map/ppermute | solution.py:25
  68.0 25.4 %collective-permute-start.31 = (bf16[2,4,32,2048]{3,2,1,0:T(8,128)(2,1)S(1)}, bf16[2,4,32,2048]{3,2,1,0:T(8,128)(2,1)}, u32[]{:S(2)}, u32[]{:S(2)}) collective-permute-start(bf16[2,4,32,2048]{3,2,1,0:T(8,128)(2,1)S(1)} %bitcast.111), channel_id=1, source_target_pairs={{0,16},{16,32},{32,48},{48,0},{1,17},{17,33},{33,49},{49,1},{2,18}... | collective-permute-start | bytes 3145736 | tf_op jit(solution)/shard_map/ppermute | solution.py:25
  72.0 23.4 %collective-permute-start.21 = (bf16[16,1280]{1,0:T(8,128)(2,1)S(1)}, bf16[16,1280]{1,0:T(8,128)(2,1)S(1)}, u32[]{:S(2)}, u32[]{:S(2)}) collective-permute-start(bf16[16,1280]{1,0:T(8,128)(2,1)S(1)} %get-tuple-element.28), channel_id=1, source_target_pairs={{0,1},{1,64},{64,65},{65,0},{2,3},{3,66},{66,67},{67,2},{4,5},{5,6... | collective-permute-start | bytes 122888 | tf_op jit(solution)/shard_map/ppermute | solution.py:25
  91.0 5.5 %collective-permute-start.20 = (bf16[16,1280]{1,0:T(8,128)(2,1)S(1)}, bf16[16,1280]{1,0:T(8,128)(2,1)S(1)}, u32[]{:S(2)}, u32[]{:S(2)}) collective-permute-start(bf16[16,1280]{1,0:T(8,128)(2,1)S(1)} %get-tuple-element.28), channel_id=1, source_target_pairs={{0,64},{1,65},{64,0},{65,1},{2,66},{3,67},{66,2},{67,3},{4,68},{5,... | collective-permute-start | bytes 122888 | tf_op jit(solution)/shard_map/ppermute | solution.py:25
  93.4 5.4 %collective-permute-start.19 = (bf16[16,1280]{1,0:T(8,128)(2,1)S(1)}, bf16[16,1280]{1,0:T(8,128)(2,1)S(1)}, u32[]{:S(2)}, u32[]{:S(2)}) collective-permute-start(bf16[16,1280]{1,0:T(8,128)(2,1)S(1)} %get-tuple-element.28), channel_id=1, source_target_pairs={{0,65},{1,0},{64,1},{65,64},{2,67},{3,2},{66,3},{67,66},{4,69},{5,... | collective-permute-start | bytes 122888 | tf_op jit(solution)/shard_map/ppermute | solution.py:25
  95.5 5.3 %collective-permute-start.3 = (bf16[16,1408]{1,0:T(8,128)(2,1)S(1)}, bf16[16,1408]{1,0:T(8,128)(2,1)S(1)}, u32[]{:S(2)}, u32[]{:S(2)}) collective-permute-start(bf16[16,1408]{1,0:T(8,128)(2,1)S(1)} %get-tuple-element.32), channel_id=1, source_target_pairs={{0,16},{16,32},{32,48},{48,0},{1,17},{17,33},{33,49},{49,1},{2,18}... | collective-permute-start | bytes 135176 | tf_op jit(solution)/shard_map/ppermute | solution.py:25
  96.5 6.0 %collective-permute-start.2 = (bf16[16,1408]{1,0:T(8,128)(2,1)S(1)}, bf16[16,1408]{1,0:T(8,128)(2,1)S(1)}, u32[]{:S(2)}, u32[]{:S(2)}) collective-permute-start(bf16[16,1408]{1,0:T(8,128)(2,1)S(1)} %get-tuple-element.32), channel_id=1, source_target_pairs={{0,32},{16,48},{32,0},{48,16},{1,33},{17,49},{33,1},{49,17},{2,34}... | collective-permute-start | bytes 135176 | tf_op jit(solution)/shard_map/ppermute | solution.py:25
  98.7 7.3 %collective-permute-start.1 = (bf16[16,1408]{1,0:T(8,128)(2,1)S(1)}, bf16[16,1408]{1,0:T(8,128)(2,1)S(1)}, u32[]{:S(2)}, u32[]{:S(2)}) collective-permute-start(bf16[16,1408]{1,0:T(8,128)(2,1)S(1)} %get-tuple-element.32), channel_id=1, source_target_pairs={{0,48},{16,0},{32,16},{48,32},{1,49},{17,1},{33,17},{49,33},{2,50}... | collective-permute-start | bytes 135176 | tf_op jit(solution)/shard_map/ppermute | solution.py:25
  100.8 6.5 %collective-permute-start.12 = (bf16[16,1408]{1,0:T(8,128)(2,1)S(1)}, bf16[16,1408]{1,0:T(8,128)(2,1)S(1)}, u32[]{:S(2)}, u32[]{:S(2)}) collective-permute-start(bf16[16,1408]{1,0:T(8,128)(2,1)S(1)} %get-tuple-element.31), channel_id=1, source_target_pairs={{0,2},{2,4},{4,6},{6,0},{1,3},{3,5},{5,7},{7,1},{8,10},{10,12},{12... | collective-permute-start | bytes 135176 | tf_op jit(solution)/shard_map/ppermute | solution.py:25
  102.5 7.6 %collective-permute-start.11 = (bf16[16,1408]{1,0:T(8,128)(2,1)S(1)}, bf16[16,1408]{1,0:T(8,128)(2,1)S(1)}, u32[]{:S(2)}, u32[]{:S(2)}) collective-permute-start(bf16[16,1408]{1,0:T(8,128)(2,1)S(1)} %get-tuple-element.31), channel_id=1, source_target_pairs={{0,4},{2,6},{4,0},{6,2},{1,5},{3,7},{5,1},{7,3},{8,12},{10,14},{12... | collective-permute-start | bytes 135176 | tf_op jit(solution)/shard_map/ppermute | solution.py:25
  106.0 7.9 %collective-permute-start.24 = (bf16[4,16,1280]{2,1,0:T(8,128)(2,1)S(1)}, bf16[4,16,1280]{2,1,0:T(8,128)(2,1)S(1)}, u32[]{:S(2)}, u32[]{:S(2)}) collective-permute-start(bf16[4,16,1280]{2,1,0:T(8,128)(2,1)S(1)} %get-tuple-element.26), channel_id=1, source_target_pairs={{0,2},{2,4},{4,6},{6,0},{1,3},{3,5},{5,7},{7,1},{8,10},{10,12},{12... | collective-permute-start | bytes 491528 | tf_op jit(solution)/shard_map/ppermute | solution.py:25
  107.4 18.0 %collective-permute-start.32 = (bf16[4,32,2048]{2,1,0:T(8,128)(2,1)S(1)}, bf16[4,32,2048]{2,1,0:T(8,128)(2,1)S(1)}, u32[]{:S(2)}, u32[]{:S(2)}) collective-permute-start(bf16[4,32,2048]{2,1,0:T(8,128)(2,1)S(1)} %slice_bitcast_fusion.1), channel_id=1, source_target_pairs={{0,48},{16,0},{32,16},{48,32},{1,49},{17,1},{33,17},{49,33},{2,50}... | collective-permute-start | bytes 1572872 | tf_op jit(solution)/shard_map/ppermute | solution.py:25
  110.1 6.8 %collective-permute-start.23 = (bf16[4,16,1280]{2,1,0:T(8,128)(2,1)S(1)}, bf16[4,16,1280]{2,1,0:T(8,128)(2,1)S(1)}, u32[]{:S(2)}, u32[]{:S(2)}) collective-permute-start(bf16[4,16,1280]{2,1,0:T(8,128)(2,1)S(1)} %get-tuple-element.26), channel_id=1, source_target_pairs={{0,4},{2,6},{4,0},{6,2},{1,5},{3,7},{5,1},{7,3},{8,12},{10,14},{12... | collective-permute-start | bytes 491528 | tf_op jit(solution)/shard_map/ppermute | solution.py:25
  113.9 5.5 %collective-permute-start.22 = (bf16[4,16,1280]{2,1,0:T(8,128)(2,1)S(1)}, bf16[4,16,1280]{2,1,0:T(8,128)(2,1)S(1)}, u32[]{:S(2)}, u32[]{:S(2)}) collective-permute-start(bf16[4,16,1280]{2,1,0:T(8,128)(2,1)S(1)} %get-tuple-element.26), channel_id=1, source_target_pairs={{0,6},{2,0},{4,2},{6,4},{1,7},{3,1},{5,3},{7,5},{8,14},{10,8},{12,... | collective-permute-start | bytes 491528 | tf_op jit(solution)/shard_map/ppermute | solution.py:25
  116.9 11.5 %collective-permute-start.33 = (bf16[4,32,2048]{2,1,0:T(8,128)(2,1)S(1)}, bf16[4,32,2048]{2,1,0:T(8,128)(2,1)S(1)}, u32[]{:S(2)}, u32[]{:S(2)}) collective-permute-start(bf16[4,32,2048]{2,1,0:T(8,128)(2,1)S(1)} %slice_bitcast_fusion), channel_id=1, source_target_pairs={{0,16},{16,32},{32,48},{48,0},{1,17},{17,33},{33,49},{49,1},{2,18}... | collective-permute-start | bytes 1572872 | tf_op jit(solution)/shard_map/ppermute | solution.py:25
  119.5 4.4 %collective-permute-start.10 = (bf16[16,1408]{1,0:T(8,128)(2,1)S(1)}, bf16[16,1408]{1,0:T(8,128)(2,1)S(1)}, u32[]{:S(2)}, u32[]{:S(2)}) collective-permute-start(bf16[16,1408]{1,0:T(8,128)(2,1)S(1)} %get-tuple-element.31), channel_id=1, source_target_pairs={{0,6},{2,0},{4,2},{6,4},{1,7},{3,1},{5,3},{7,5},{8,14},{10,8},{12,... | collective-permute-start | bytes 135176 | tf_op jit(solution)/shard_map/ppermute | solution.py:25
  122.2 24.0 %copy-start.5 = (bf16[4,4,16,1280]{3,2,1,0:T(8,128)(2,1)}, bf16[4,4,16,1280]{3,2,1,0:T(8,128)(2,1)S(1)}, u32[]{:S(2)}) copy-start(bf16[4,4,16,1280]{3,2,1,0:T(8,128)(2,1)S(1)} %pad_maximum_fusion.3.refs_8_) | copy-start | bytes 1966084
  123.8 22.3 %collective-permute-start.25 = (bf16[4,4,16,1280]{3,2,1,0:T(8,128)(2,1)S(1)}, bf16[4,4,16,1280]{3,2,1,0:T(8,128)(2,1)S(1)}, u32[]{:S(2)}, u32[]{:S(2)}) collective-permute-start(bf16[4,4,16,1280]{3,2,1,0:T(8,128)(2,1)S(1)} %pad_maximum_fusion.3.refs_8_), channel_id=1, source_target_pairs={{0,48},{16,0},{32,16},{48,32},{1,49},{17,1},{33,17},{49,33},{2,50}... | collective-permute-start | bytes 1966088 | tf_op jit(solution)/shard_map/ppermute | solution.py:25
  125.3 13.3 %copy-start.17 = (bf16[4,32,2048]{2,1,0:T(8,128)(2,1)}, bf16[4,32,2048]{2,1,0:T(8,128)(2,1)S(1)}, u32[]{:S(2)}) copy-start(bf16[4,32,2048]{2,1,0:T(8,128)(2,1)S(1)} %collective-permute-done.32.refs_3_) | copy-start | bytes 1572868
  125.4 6.8 %collective-permute-start.6 = (bf16[4,16,1408]{2,1,0:T(8,128)(2,1)S(1)}, bf16[4,16,1408]{2,1,0:T(8,128)(2,1)S(1)}, u32[]{:S(2)}, u32[]{:S(2)}) collective-permute-start(bf16[4,16,1408]{2,1,0:T(8,128)(2,1)S(1)} %get-tuple-element.24), channel_id=1, source_target_pairs={{0,1},{1,64},{64,65},{65,0},{2,3},{3,66},{66,67},{67,2},{4,5},{5,6... | collective-permute-start | bytes 540680 | tf_op jit(solution)/shard_map/ppermute | solution.py:25
  128.4 10.2 %copy-start.19 = (bf16[4,32,2048]{2,1,0:T(8,128)(2,1)}, bf16[4,32,2048]{2,1,0:T(8,128)(2,1)S(1)}, u32[]{:S(2)}) copy-start(bf16[4,32,2048]{2,1,0:T(8,128)(2,1)S(1)} %collective-permute-done.33.refs_4_) | copy-start | bytes 1572868
  128.4 7.0 %collective-permute-start.5 = (bf16[4,16,1408]{2,1,0:T(8,128)(2,1)S(1)}, bf16[4,16,1408]{2,1,0:T(8,128)(2,1)S(1)}, u32[]{:S(2)}, u32[]{:S(2)}) collective-permute-start(bf16[4,16,1408]{2,1,0:T(8,128)(2,1)S(1)} %get-tuple-element.24), channel_id=1, source_target_pairs={{0,64},{1,65},{64,0},{65,1},{2,66},{3,67},{66,2},{67,3},{4,68},{5,... | collective-permute-start | bytes 540680 | tf_op jit(solution)/shard_map/ppermute | solution.py:25
  130.2 6.8 %collective-permute-start.4 = (bf16[4,16,1408]{2,1,0:T(8,128)(2,1)S(1)}, bf16[4,16,1408]{2,1,0:T(8,128)(2,1)S(1)}, u32[]{:S(2)}, u32[]{:S(2)}) collective-permute-start(bf16[4,16,1408]{2,1,0:T(8,128)(2,1)S(1)} %get-tuple-element.24), channel_id=1, source_target_pairs={{0,65},{1,0},{64,1},{65,64},{2,67},{3,2},{66,3},{67,66},{4,69},{5,... | collective-permute-start | bytes 540680 | tf_op jit(solution)/shard_map/ppermute | solution.py:25
  132.1 6.7 %collective-permute-start.15 = (bf16[4,16,1408]{2,1,0:T(8,128)(2,1)S(1)}, bf16[4,16,1408]{2,1,0:T(8,128)(2,1)S(1)}, u32[]{:S(2)}, u32[]{:S(2)}) collective-permute-start(bf16[4,16,1408]{2,1,0:T(8,128)(2,1)S(1)} %get-tuple-element.22), channel_id=1, source_target_pairs={{0,16},{16,32},{32,48},{48,0},{1,17},{17,33},{33,49},{49,1},{2,18}... | collective-permute-start | bytes 540680 | tf_op jit(solution)/shard_map/ppermute | solution.py:25
  135.4 7.0 %collective-permute-start.14 = (bf16[4,16,1408]{2,1,0:T(8,128)(2,1)S(1)}, bf16[4,16,1408]{2,1,0:T(8,128)(2,1)S(1)}, u32[]{:S(2)}, u32[]{:S(2)}) collective-permute-start(bf16[4,16,1408]{2,1,0:T(8,128)(2,1)S(1)} %get-tuple-element.22), channel_id=1, source_target_pairs={{0,32},{16,48},{32,0},{48,16},{1,33},{17,49},{33,1},{49,17},{2,34}... | collective-permute-start | bytes 540680 | tf_op jit(solution)/shard_map/ppermute | solution.py:25
  137.0 6.9 %collective-permute-start.13 = (bf16[4,16,1408]{2,1,0:T(8,128)(2,1)S(1)}, bf16[4,16,1408]{2,1,0:T(8,128)(2,1)S(1)}, u32[]{:S(2)}, u32[]{:S(2)}) collective-permute-start(bf16[4,16,1408]{2,1,0:T(8,128)(2,1)S(1)} %get-tuple-element.22), channel_id=1, source_target_pairs={{0,48},{16,0},{32,16},{48,32},{1,49},{17,1},{33,17},{49,33},{2,50}... | collective-permute-start | bytes 540680 | tf_op jit(solution)/shard_map/ppermute | solution.py:25
  138.8 35.7 %collective-permute-start.7 = (bf16[4,4,16,1408]{3,2,1,0:T(8,128)(2,1)}, bf16[4,4,16,1408]{3,2,1,0:T(8,128)(2,1)S(1)}, u32[]{:S(2)}, u32[]{:S(2)}) collective-permute-start(bf16[4,4,16,1408]{3,2,1,0:T(8,128)(2,1)} %pad_maximum_fusion.1.refs_0_), channel_id=1, source_target_pairs={{0,6},{2,0},{4,2},{6,4},{1,7},{3,1},{5,3},{7,5},{8,14},{10,8},{12,... | collective-permute-start | bytes 2162696 | tf_op jit(solution)/shard_map/ppermute | solution.py:25
  142.4 33.5 %collective-permute-start.8 = (bf16[4,4,16,1408]{3,2,1,0:T(8,128)(2,1)}, bf16[4,4,16,1408]{3,2,1,0:T(8,128)(2,1)S(1)}, u32[]{:S(2)}, u32[]{:S(2)}) collective-permute-start(bf16[4,4,16,1408]{3,2,1,0:T(8,128)(2,1)} %pad_maximum_fusion.1.refs_0_), channel_id=1, source_target_pairs={{0,4},{2,6},{4,0},{6,2},{1,5},{3,7},{5,1},{7,3},{8,12},{10,14},{12... | collective-permute-start | bytes 2162696 | tf_op jit(solution)/shard_map/ppermute | solution.py:25
  143.9 19.1 %collective-permute-start.26 = (bf16[4,4,16,1280]{3,2,1,0:T(8,128)(2,1)S(1)}, bf16[4,4,16,1280]{3,2,1,0:T(8,128)(2,1)S(1)}, u32[]{:S(2)}, u32[]{:S(2)}) collective-permute-start(bf16[4,4,16,1280]{3,2,1,0:T(8,128)(2,1)S(1)} %pad_maximum_fusion.3.refs_8_), channel_id=1, source_target_pairs={{0,32},{16,48},{32,0},{48,16},{1,33},{17,49},{33,1},{49,17},{2,34}... | collective-permute-start | bytes 1966088 | tf_op jit(solution)/shard_map/ppermute | solution.py:25
  146.2 29.7 %copy-start.11 = (bf16[4,4,16,1280]{3,2,1,0:T(8,128)(2,1)}, bf16[4,4,16,1280]{3,2,1,0:T(8,128)(2,1)S(1)}, u32[]{:S(2)}) copy-start(bf16[4,4,16,1280]{3,2,1,0:T(8,128)(2,1)S(1)} %collective-permute-done.25.refs_9_) | copy-start | bytes 1966084
  146.2 25.0 %collective-permute-start.27 = (bf16[4,4,16,1280]{3,2,1,0:T(8,128)(2,1)S(1)}, bf16[4,4,16,1280]{3,2,1,0:T(8,128)(2,1)S(1)}, u32[]{:S(2)}, u32[]{:S(2)}) collective-permute-start(bf16[4,4,16,1280]{3,2,1,0:T(8,128)(2,1)S(1)} %pad_maximum_fusion.3.refs_8_), channel_id=1, source_target_pairs={{0,16},{16,32},{32,48},{48,0},{1,17},{17,33},{33,49},{49,1},{2,18}... | collective-permute-start | bytes 1966088 | tf_op jit(solution)/shard_map/ppermute | solution.py:25
  163.9 26.6 %collective-permute-start.9 = (bf16[4,4,16,1408]{3,2,1,0:T(8,128)(2,1)}, bf16[4,4,16,1408]{3,2,1,0:T(8,128)(2,1)}, u32[]{:S(2)}, u32[]{:S(2)}) collective-permute-start(bf16[4,4,16,1408]{3,2,1,0:T(8,128)(2,1)} %pad_maximum_fusion.1.refs_0_), channel_id=1, source_target_pairs={{0,2},{2,4},{4,6},{6,0},{1,3},{3,5},{5,7},{7,1},{8,10},{10,12},{12... | collective-permute-start | bytes 2162696 | tf_op jit(solution)/shard_map/ppermute | solution.py:25
  172.0 34.0 %collective-permute-start.16 = (bf16[4,4,16,1408]{3,2,1,0:T(8,128)(2,1)}, bf16[4,4,16,1408]{3,2,1,0:T(8,128)(2,1)}, u32[]{:S(2)}, u32[]{:S(2)}) collective-permute-start(bf16[4,4,16,1408]{3,2,1,0:T(8,128)(2,1)} %pad_maximum_fusion.2.refs_4_), channel_id=1, source_target_pairs={{0,65},{1,0},{64,1},{65,64},{2,67},{3,2},{66,3},{67,66},{4,69},{5,... | collective-permute-start | bytes 2162696 | tf_op jit(solution)/shard_map/ppermute | solution.py:25
  175.4 30.6 %collective-permute-start.17 = (bf16[4,4,16,1408]{3,2,1,0:T(8,128)(2,1)}, bf16[4,4,16,1408]{3,2,1,0:T(8,128)(2,1)}, u32[]{:S(2)}, u32[]{:S(2)}) collective-permute-start(bf16[4,4,16,1408]{3,2,1,0:T(8,128)(2,1)} %pad_maximum_fusion.2.refs_4_), channel_id=1, source_target_pairs={{0,64},{1,65},{64,0},{65,1},{2,66},{3,67},{66,2},{67,3},{4,68},{5,... | collective-permute-start | bytes 2162696 | tf_op jit(solution)/shard_map/ppermute | solution.py:25
  176.7 33.8 %collective-permute-start.18 = (bf16[4,4,16,1408]{3,2,1,0:T(8,128)(2,1)}, bf16[4,4,16,1408]{3,2,1,0:T(8,128)(2,1)}, u32[]{:S(2)}, u32[]{:S(2)}) collective-permute-start(bf16[4,4,16,1408]{3,2,1,0:T(8,128)(2,1)} %pad_maximum_fusion.2.refs_4_), channel_id=1, source_target_pairs={{0,1},{1,64},{64,65},{65,0},{2,3},{3,66},{66,67},{67,2},{4,5},{5,6... | collective-permute-start | bytes 2162696 | tf_op jit(solution)/shard_map/ppermute | solution.py:25
  177.2 1.0 copy-start.18
  178.2 1.0 copy-start.20
  179.3 31.3 %copy-start.6 = (bf16[4,4,16,1280]{3,2,1,0:T(8,128)(2,1)S(1)}, bf16[4,4,16,1280]{3,2,1,0:T(8,128)(2,1)}, u32[]{:S(2)}) copy-start(bf16[4,4,16,1280]{3,2,1,0:T(8,128)(2,1)} %copy-done.5) | copy-start | bytes 1966084
  179.3 31.3 %copy-start.8 = (bf16[4,4,16,1408]{3,2,1,0:T(8,128)(2,1)S(1)}, bf16[4,4,16,1408]{3,2,1,0:T(8,128)(2,1)}, u32[]{:S(2)}) copy-start(bf16[4,4,16,1408]{3,2,1,0:T(8,128)(2,1)} %copy-done.7) | copy-start | bytes 2162692
  179.3 31.3 %copy-start.10 = (bf16[4,4,16,1408]{3,2,1,0:T(8,128)(2,1)S(1)}, bf16[4,4,16,1408]{3,2,1,0:T(8,128)(2,1)}, u32[]{:S(2)}) copy-start(bf16[4,4,16,1408]{3,2,1,0:T(8,128)(2,1)} %copy-done.9) | copy-start | bytes 2162692
  179.3 31.3 %copy-start.12 = (bf16[4,4,16,1280]{3,2,1,0:T(8,128)(2,1)S(1)}, bf16[4,4,16,1280]{3,2,1,0:T(8,128)(2,1)}, u32[]{:S(2)}) copy-start(bf16[4,4,16,1280]{3,2,1,0:T(8,128)(2,1)} %copy-done.11) | copy-start | bytes 1966084
  179.3 31.3 %copy-start.14 = (bf16[4,4,16,1280]{3,2,1,0:T(8,128)(2,1)S(1)}, bf16[4,4,16,1280]{3,2,1,0:T(8,128)(2,1)}, u32[]{:S(2)}) copy-start(bf16[4,4,16,1280]{3,2,1,0:T(8,128)(2,1)} %copy-done.13) | copy-start | bytes 1966084
  179.3 31.3 %copy-start.16 = (bf16[4,4,16,1280]{3,2,1,0:T(8,128)(2,1)S(1)}, bf16[4,4,16,1280]{3,2,1,0:T(8,128)(2,1)}, u32[]{:S(2)}) copy-start(bf16[4,4,16,1280]{3,2,1,0:T(8,128)(2,1)} %copy-done.15) | copy-start | bytes 1966084
  188.4 2.0 copy-start.2
  210.6 20.4 %copy-start.26 = (s32[2048]{0:T(1024)S(1)}, s32[2048]{0:T(1024)}, u32[]{:S(2)}) copy-start(s32[2048]{0:T(1024)} %param.23) | copy-start | bytes 24580
  227.6 9.8 %all-to-all-start.2 = ((f32[8,4,1024]{2,1,0:T(4,128)}), f32[8,4,1024]{2,1,0:T(4,128)S(1)}, u32[]{:S(2)}, u32[]{:S(2)}) async-start(f32[8,4,1024]{2,1,0:T(4,128)} %broadcast_in_dim.56), calls=%async_computation.2 | async-start | bytes 262144 | tf_op jit(solution)/shard_map/all_to_all | solution.py:420
  238.5 12.6 %all-to-all-start.3 = ((f32[8,4,1024]{2,1,0:T(4,128)}), f32[8,4,1024]{2,1,0:T(4,128)S(1)}, u32[]{:S(2)}, u32[]{:S(2)}) async-start(f32[8,4,1024]{2,1,0:T(4,128)} %broadcast_in_dim.57), calls=%async_computation.3 | async-start | bytes 262144 | tf_op jit(solution)/shard_map/all_to_all | solution.py:420
  251.6 2.2 copy-start.3
  263.3 55.4 %copy-start.1 = (bf16[4096,128]{1,0:T(8,128)(2,1)S(1)}, bf16[4096,128]{1,0:T(8,128)(2,1)}, u32[]{:S(2)}) copy-start(bf16[4096,128]{1,0:T(8,128)(2,1)} %param.17) | copy-start | bytes 3145732
  (5 other events, 4.2 us)
where the time goes:
time: 320 us; the launch traced here: 319 us
  waiting for transfers between devices  119 us (37%)
  starting transfers between devices  67.9 us (21%)
  blocking collectives  54.2 us (17%)
  Pallas kernels  34.9 us (11%)
  local copies, waits for them, and re-layouts  17.2 us (5%)
  other arithmetic  14.5 us (5%)
  matrix products  10.7 us (3%)
    ppermute x35, waiting for transfers between devices, shifted(): return lax.ppermute(a, axes, [(i, (i + k) % n) for i in range(n)])  97.7 us
    all_to_all x1, blocking collectives, on_device(): lax.all_to_all(parts, CHIPS, split_axis=0, concat_axis=0, tiled=True)  54.2 us
    ppermute x35, starting transfers between devices, shifted(): return lax.ppermute(a, axes, [(i, (i + k) % n) for i in range(n)])  47.3 us
    pallas_call x1, Pallas kernels, teacher_logits(): pl.pallas_call(teacher_kernel, grid_spec=pltpu.PrefetchScalarGridSpec(num...  16.3 us
    all_to_all x2, waiting for transfers between devices, on_device(): lax.all_to_all(copies, axes, split_axis=0, concat_axis=0, tiled=True)  14.2 us
    unnamed x60, local copies, waits for them, and re-layouts  11.6 us
    pallas_call x1, Pallas kernels, gradient_parts(): pl.pallas_call(gradient_kernel, grid_spec=pltpu.PrefetchScalarGridSpec(nu...  9.51 us
    pallas_call x1, Pallas kernels, draft_logits(): pl.pallas_call(draft_kernel, grid_spec=pltpu.PrefetchScalarGridSpec(num_s...  9.11 us
  transfers between devices with their start and end apart: 39, of which 23 were waited for; matrix products, arithmetic and copies ran while one was open for 5% of the time, Pallas kernels for 3%

commit v1 on v0

--- a/solution.py
+++ b/solution.py
@@ -15,7 +15,7 @@
 
 CTX = ("yh", "z", "c")
 VOCAB = ("x", "yl")
-X, Y, Z, C = ("x",), ("yh", "yl"), ("z",), ("c",)
+Z, C = ("z",), ("c",)
 CHIPS = ("yh", "z", "x", "yl")
 F32, BF16 = jnp.float32, jnp.bfloat16
 
@@ -28,6 +28,26 @@
 def ring(a, axes):
     n = lax.axis_size(axes)
     return [a] + [shifted(a, axes, n - d) for d in range(1, n)]
+
+
+EVERY = ("yh", "z", "c", "x", "yl")
+
+
+def moved(a, along, k):
+    pairs = []
+    for source in range(128):
+        yh, z, c = source // 64, source // 16 % 4, source // 8 % 2
+        x, yl = source // 2 % 4, source % 2
+        y = 2 * yh + yl
+        x = (x + k) % 4 if along[c] == "x" else x
+        y = (y + k) % 4 if along[c] == "y" else y
+        z = (z + k) % 4 if along[c] == "z" else z
+        pairs.append((source, (((y // 2 * 4 + z) * 2 + c) * 4 + x) * 2 + y % 2))
+    return lax.ppermute(a, EVERY, pairs)
+
+
+def spread(a, along):
+    return [a] + [moved(a, along, 4 - d) for d in range(1, 4)]
 
 
 def rms_scale(values, gain):
@@ -131,22 +151,18 @@
 
 
 def draft_kernel(place, *refs):
-    near_ref, ahead_ref, behind_ref = refs[0:3]
-    own_ref, other_ref, out_ref, stats_ref, x_ref, held_ref, arrived, top_ref, sum_ref = refs[5:]
+    row_refs = refs[0:8]
+    own_ref, other_ref, out_ref, stats_ref, x_ref, held_ref, arrived, top_ref, sum_ref = refs[8:]
     slot = fetch_words(own_ref, other_ref, held_ref, arrived)
 
     @pl.when(pl.program_id(0) == 0)
     def _():
-        for dz in range(4):
-            pz = (place[2] + dz) % 4
-            for dyh in range(2):
-                base = (place[1] // 2 + dyh) % 2 * 128 + pz * 32
+        for dyh in range(2):
+            for dz in range(4):
+                base = place[12 + dyh] + place[8 + dz]
                 for x in range(4):
                     at = pl.ds(pl.multiple_of(base + x * 256, 32), 32)
-                    if dz == 2:
-                        x_ref[at, :] = refs[3 + dyh][x]
-                    else:
-                        x_ref[at, :] = (near_ref, ahead_ref, None, behind_ref)[dz][dyh, x]
+                    x_ref[at, :] = row_refs[dyh * 4 + dz][x]
 
     logits_step(slot, x_ref, held_ref, out_ref, top_ref, sum_ref)
 
@@ -187,25 +203,21 @@
 
 
 def teacher_kernel(place, *refs):
-    a_refs, b_refs, c_refs = refs[0:4], refs[4:8], refs[8:12]
-    own_ref, other_ref, draft_stats, out_ref, stats_ref = refs[12:17]
-    x_ref, held_ref, arrived, top_ref, sum_ref = refs[17:]
+    p_refs, q_refs = refs[0:4], refs[4:8]
+    own_ref, other_ref, draft_stats, out_ref, stats_ref = refs[8:13]
+    x_ref, held_ref, arrived, top_ref, sum_ref = refs[13:]
     slot = fetch_words(own_ref, other_ref, held_ref, arrived)
 
     @pl.when(pl.program_id(0) == 0)
     def _():
-        a_width, b_width = a_refs[0].shape[-1], b_refs[0].shape[-1]
-        for dx in range(4):
-            px = (place[0] + dx) % 4
-            for dy in range(4):
-                py = (place[1] + dy) % 4
-                for dz in range(4):
-                    pz = (place[2] + dz) % 4
-                    row = px * 256 + (py // 2) * 128 + pz * 32 + (py % 2) * 16
-                    at = pl.ds(pl.multiple_of(row, 16), 16)
-                    x_ref[at, :a_width] = a_refs[dx][dy, dz]
-                    x_ref[at, a_width : a_width + b_width] = b_refs[dy][dz, dx]
-                    x_ref[at, a_width + b_width :] = c_refs[dz][dx, dy]
+        cut = p_refs[0].shape[-1]
+        for k in range(4):
+            for i in range(4):
+                for j in range(4):
+                    row = place[k] + place[4 + i] + place[8 + j]
+                    x_ref[pl.ds(pl.multiple_of(row, 16), 16), :cut] = p_refs[k][i, j]
+                    row = place[8 + k] + place[4 + i] + place[j]
+                    x_ref[pl.ds(pl.multiple_of(row, 16), 16), cut:] = q_refs[k][i, j]
 
     logits_step(slot, x_ref, held_ref, out_ref, top_ref, sum_ref)
 
@@ -339,9 +351,9 @@
     both = jnp.concatenate([keys, values], axis=1)
     copies = jnp.broadcast_to(both[None], (8, *both.shape))
     both = lax.all_to_all(copies, ("yh", "z"), split_axis=0, concat_axis=0, tiled=True)
-    gathered = both
     both = both.reshape(8 * row_count, -1)
-    both = jnp.concatenate(ring(both, C), axis=0)
+    both = ring(both, C)
+    both = jnp.concatenate(both, axis=0)
     key_width = local_groups * head_dim
     key_piece = both[:, :key_width].reshape(-1, local_groups, head_dim)
     value_piece = both[:, key_width:].reshape(-1, local_groups, head_dim)
@@ -394,33 +406,50 @@
     teacher_other = shifted(teacher_head, C, 1)
     draft_other = shifted(draft_head, C, 1)
 
-    place = jnp.stack([my_x, my_yh * 2 + my_yl, my_z]).astype(jnp.int32)
-    near = jnp.stack(ring(draft_rows, ("yh",)))
-    near, _ = lax.optimization_barrier((near, gathered))
-    near = near.reshape(2, 4, 2 * share_rows, -1)
-    ahead, behind = shifted(near, Z, 3), shifted(near, Z, 1)
-    far = [shifted(ahead[0], Z, 3), shifted(behind[1], Z, 1)]
+    turns = jnp.arange(4, dtype=jnp.int32)
+    at_x, at_z = (my_x + turns) % 4 * 256, (my_z + turns) % 4 * 32
+    at_y = (my_yh * 2 + my_yl + turns) % 4
+    at_y = at_y // 2 * 128 + at_y % 2 * 16
+    even = my_c == 0
+    place = jnp.concatenate(
+        [
+            jnp.where(even, at_x, at_y),
+            jnp.where(even, at_y, at_x),
+            at_z,
+            (my_yh + turns) % 2 * 128,
+        ]
+    )
+    here = draft_rows.reshape(4, 2 * share_rows, -1)
+    there = shifted(here, ("yh",), 1)
+    ahead, behind = shifted(here, Z, 3), shifted(here, Z, 1)
+    ahead_there, behind_there = shifted(there, Z, 3), shifted(there, Z, 1)
+    far, far_there = shifted(ahead, Z, 3), shifted(behind_there, Z, 1)
     draft_part, draft_stats = draft_logits(
-        place, [near, ahead, behind] + far, draft_head, draft_other
-    )
-
-    a, b, c = jnp.split(final, [1408, 2816], axis=1)
-    a, b, c = ring(a, Z), ring(b, X), ring(c, Y)
-    a, b, c = jnp.stack(a), jnp.stack(b), jnp.stack(c)
-    a = jnp.stack(ring(a, Y))
-    b = jnp.stack(ring(b, Z))
-    c = jnp.stack(ring(c, X))
-    a, b, c = ring(a, X), ring(b, Y), ring(c, Z)
-    teacher_part, stats = teacher_logits(
-        place, a + b + c, teacher_head, teacher_other, draft_stats
-    )
+        place,
+        [here, ahead, far, behind, there, ahead_there, far_there, behind_there],
+        draft_head,
+        draft_other,
+    )
+
+    p, q = jnp.split(final, [2560], axis=1)
+    p = spread(p, "zz")
+    q = spread(q, "xy")
+    p, q = jnp.stack(p), jnp.stack(q)
+    p = spread(p, "yx")
+    q = spread(q, "yx")
+    p, q = jnp.stack(p), jnp.stack(q)
+    p = spread(p, "xy")
+    q = spread(q, "zz")
+    teacher_part, stats = teacher_logits(place, p + q, teacher_head, teacher_other, draft_stats)
+
+    def merged(pieces):
+        tops = jnp.max(pieces[:, 0::2], axis=0)
+        sums = jnp.sum(pieces[:, 1::2] * jnp.exp(pieces[:, 0::2] - tops), axis=0)
+        return jnp.stack([tops[0], sums[0], tops[1], sums[1]])
 
     for axes in (("x", "yl"), ("yh", "z")):
         copies = jnp.broadcast_to(stats[None, :4], (8, *stats[:4].shape))
-        pieces = lax.all_to_all(copies, axes, split_axis=0, concat_axis=0, tiled=True)
-        tops = jnp.max(pieces[:, 0::2], axis=0)
-        sums = jnp.sum(pieces[:, 1::2] * jnp.exp(pieces[:, 0::2] - tops), axis=0)
-        stats = jnp.stack([tops[0], sums[0], tops[1], sums[1]])
+        stats = merged(lax.all_to_all(copies, axes, split_axis=0, concat_axis=0, tiled=True))
     targets = target_ids.reshape(2, 4, 2, 4, 2 * share_rows)
     targets = lax.dynamic_index_in_dim(targets, my_c, 2, keepdims=False)
     targets = jnp.transpose(targets, (2, 0, 1, 3)).reshape(-1).astype(F32)

time: 320 us -> 281 us (0.88)
  waiting for transfers between devices: 119 us -> 86.2 us
  blocking collectives: 54.2 us -> 41.2 us
  local copies, waits for them, and re-layouts: 17.2 us -> 23.7 us
    ppermute x35 -> x10, waiting for transfers between devices: 97.7 us -> 31.3 us  [shifted(): return lax.ppermute(a, axes, [(i, (i + k) % n) for i in range(n)])]
    ppermute x35 -> x10, starting transfers between devices: 47.3 us -> 8.9 us  [shifted(): return lax.ppermute(a, axes, [(i, (i + k) % n) for i in range(n)])]
    ppermute x0 -> x18, starting transfers between devices: none -> 31.6 us  [moved(): return lax.ppermute(a, EVERY, pairs)]
    ppermute x0 -> x18, waiting for transfers between devices: none -> 21 us  [moved(): return lax.ppermute(a, EVERY, pairs)]
    all_to_all x1, blocking collectives: 54.2 us -> 41.2 us  [on_device(): lax.all_to_all(parts, CHIPS, split_axis=0, concat_axis=0, tiled=True)]
    all_to_all x1, waiting for transfers between devices: 0.01 us -> 12.8 us  [on_device(): lax.all_to_all(partial_value.reshape(shares, share_rows, -1), VOCAB, spli...]
    all_to_all x2, starting transfers between devices: 7.9 us -> 18 us  [on_device(): lax.all_to_all(copies, axes, split_axis=0, concat_axis=0, tiled=True)]
    unnamed x60 -> x62, local copies, waits for them, and re-layouts: 11.6 us -> 20.3 us
  transfers between devices with their start and end apart: 39 -> 32, of which waited for: 23 -> 18; matrix products, arithmetic and copies ran while one was open for 5% -> 4% of each run, Pallas kernels for 3% -> 3%
where the time goes in v1:
time: 281 us; the launch traced here: 280 us
  waiting for transfers between devices  86.2 us (31%)
  starting transfers between devices  71.1 us (25%)
  blocking collectives  41.2 us (15%)
  Pallas kernels  34.1 us (12%)
  local copies, waits for them, and re-layouts  23.7 us (8%)
  other arithmetic  12.3 us (4%)
  matrix products  10.6 us (4%)
    all_to_all x1, blocking collectives, on_device(): lax.all_to_all(parts, CHIPS, split_axis=0, concat_axis=0, tiled=True)  41.2 us
    ppermute x18, starting transfers between devices, moved(): return lax.ppermute(a, EVERY, pairs)  31.6 us
    ppermute x10, waiting for transfers between devices, shifted(): return lax.ppermute(a, axes, [(i, (i + k) % n) for i in range(n)])  31.3 us
    ppermute x18, waiting for transfers between devices, moved(): return lax.ppermute(a, EVERY, pairs)  21 us
    unnamed x62, local copies, waits for them, and re-layouts  20.3 us
    all_to_all x2, starting transfers between devices, on_device(): lax.all_to_all(copies, axes, split_axis=0, concat_axis=0, tiled=True)  18 us
    pallas_call x1, Pallas kernels, teacher_logits(): pl.pallas_call(teacher_kernel, grid_spec=pltpu.PrefetchScalarGridSpec(num...  16.6 us
    all_to_all x2, waiting for transfers between devices, on_device(): lax.all_to_all(copies, axes, split_axis=0, concat_axis=0, tiled=True)  14.2 us
  transfers between devices with their start and end apart: 32, of which 18 were waited for; matrix products, arithmetic and copies ran while one was open for 4% of the time, Pallas kernels for 3%

profile of v1, /device:TPU:0, one launch (start us, length us, event | category | flops | bytes accessed | tf_op | source)
XLA Modules:
  0.0 279.8 jit_solution(929096391073056835)
XLA Ops:
  1.0 1.5 fusion.3
  2.5 1.8 convolution_convert_fusion.1
  4.3 2.2 convolution_bitcast_fusion
  7.7 8.2 %all-to-all-start = ((bf16[8,128,256]{2,1,0:T(8,128)(2,1)}), bf16[8,128,256]{2,1,0:T(8,128)(2,1)S(1)}, u32[]{:S(2)}, u32[]{:S(2)}) async-start(bf16[8,128,256]{2,1,0:T(8,128)(2,1)} %broadcast_in_dim.46), calls=%async_computation | async-start | bytes 1048576 | tf_op jit(solution)/shard_map/all_to_all | solution.py:353
  16.1 3.0 %fusion.77 = f32[128,512]{1,0:T(8,128)S(1)} fusion(bf16[4096,512]{1,0:T(8,128)(2,1)} %param.15, bf16[128,4096]{1,0:T(8,128)(2,1)S(1)} %copy-done.25, f32[4096]{0:T(1024)S(1)} %copy-done.29, f32[128]{0:T(128)S(1)} %add_rsqrt_fusion.1), kind=kOutput, calls=%fused_computation.157 | convolution fusion | flops 538968064 | bytes 5521920 | tf_op jit(solution)/shard_map/dot_general | solution.py:361
  20.0 6.9 %all-to-all-done = bf16[8,128,256]{2,1,0:T(8,128)(2,1)S(1)} async-done(((bf16[8,128,256]{2,1,0:T(8,128)(2,1)}), bf16[8,128,256]{2,1,0:T(8,128)(2,1)S(1)}, u32[]{:S(2)}, u32[]{:S(2)}) %all-to-all-start) | async-done | bytes 524320 | tf_op jit(solution)/shard_map/all_to_all | solution.py:353
  27.0 1.3 compare_and_fusion
  29.7 1.0 fusion.1
  30.7 1.1 fusion.16
  31.8 1.0 copy-done.24
  32.9 1.7 convolution_convert_fusion
  34.6 4.4 %all-to-all-start.1 = ((bf16[8,16,4096]{2,1,0:T(8,128)(2,1)}), bf16[8,16,4096]{2,1,0:T(8,128)(2,1)}, u32[]{:S(2)}, u32[]{:S(2)}) async-start(bf16[8,16,4096]{2,1,0:T(8,128)(2,1)} %bitcast.95), calls=%async_computation.1 | async-start | bytes 2097152 | tf_op jit(solution)/shard_map/all_to_all | solution.py:393
  39.1 1.2 collective-permute-start.20
  41.2 1.7 collective-permute-start.23
  42.9 12.8 %all-to-all-done.1 = bf16[8,16,4096]{2,1,0:T(8,128)(2,1)} async-done(((bf16[8,16,4096]{2,1,0:T(8,128)(2,1)}), bf16[8,16,4096]{2,1,0:T(8,128)(2,1)}, u32[]{:S(2)}, u32[]{:S(2)}) %all-to-all-start.1) | async-done | bytes 1048608 | tf_op jit(solution)/shard_map/all_to_all | solution.py:393
  55.7 1.4 convert_reduce_fusion.1
  57.1 1.1 multiply_reduce_fusion
  59.6 2.2 collective-permute-start.11
  61.8 3.3 %collective-permute-done.23.refs_4_ = bf16[4,32,2048]{2,1,0:T(8,128)(2,1)} collective-permute-done((bf16[4,32,2048]{2,1,0:T(8,128)(2,1)S(1)}, bf16[4,32,2048]{2,1,0:T(8,128)(2,1)}, u32[]{:S(2)}, u32[]{:S(2)}) %collective-permute-start.23) | collective-permute-done | bytes 524320 | tf_op jit(solution)/shard_map/ppermute | solution.py:25
  65.1 2.0 collective-permute-start.10
  67.1 1.5 collective-permute-start.21
  69.2 1.5 collective-permute-start.24
  70.7 1.2 collective-permute-start.15
  71.9 10.0 %collective-permute-done.21.refs_2_ = bf16[4,32,2048]{2,1,0:T(8,128)(2,1)S(1)} collective-permute-done((bf16[4,32,2048]{2,1,0:T(8,128)(2,1)S(1)}, bf16[4,32,2048]{2,1,0:T(8,128)(2,1)S(1)}, u32[]{:S(2)}, u32[]{:S(2)}) %collective-permute-start.21) | collective-permute-done | bytes 524320 | tf_op jit(solution)/shard_map/ppermute | solution.py:25
  83.6 9.0 %collective-permute-done.24.refs_5_ = bf16[4,32,2048]{2,1,0:T(8,128)(2,1)S(1)} collective-permute-done((bf16[4,32,2048]{2,1,0:T(8,128)(2,1)}, bf16[4,32,2048]{2,1,0:T(8,128)(2,1)S(1)}, u32[]{:S(2)}, u32[]{:S(2)}) %collective-permute-start.24) | collective-permute-done | bytes 524320 | tf_op jit(solution)/shard_map/ppermute | solution.py:25
  93.4 1.2 collective-permute-start.2
  94.6 2.3 collective-permute-start.1
  97.0 2.4 collective-permute-done.2
  99.4 1.2 collective-permute-start.25
  100.6 1.5 collective-permute-start.14
  102.1 2.7 collective-permute-start.13
  104.9 2.9 %collective-permute-done.14 = bf16[4,16,1536]{2,1,0:T(8,128)(2,1)S(1)} collective-permute-done((bf16[4,16,1536]{2,1,0:T(8,128)(2,1)S(1)}, bf16[4,16,1536]{2,1,0:T(8,128)(2,1)S(1)}, u32[]{:S(2)}, u32[]{:S(2)}) %collective-permute-start.14) | collective-permute-done | bytes 196640 | tf_op jit(solution)/shard_map/ppermute | solution.py:46
  107.8 1.6 collective-permute-start.6
  110.0 2.1 collective-permute-start.5
  113.1 2.6 collective-permute-start.16
  116.1 1.7 collective-permute-start.4
  117.8 2.9 %collective-permute-done.5 = bf16[4,16,2560]{2,1,0:T(8,128)(2,1)S(1)} collective-permute-done((bf16[4,16,2560]{2,1,0:T(8,128)(2,1)S(1)}, bf16[4,16,2560]{2,1,0:T(8,128)(2,1)S(1)}, u32[]{:S(2)}, u32[]{:S(2)}) %collective-permute-start.5) | collective-permute-done | bytes 327712 | tf_op jit(solution)/shard_map/ppermute | solution.py:46
  121.6 1.6 collective-permute-done.4
  123.2 3.3 %collective-permute-start.17 = (bf16[4,4,16,1536]{3,2,1,0:T(8,128)(2,1)}, bf16[4,4,16,1536]{3,2,1,0:T(8,128)(2,1)S(1)}, u32[]{:S(2)}, u32[]{:S(2)}) collective-permute-start(bf16[4,4,16,1536]{3,2,1,0:T(8,128)(2,1)} %pad_maximum_fusion.1.refs_4_), channel_id=1, source_target_pairs={{0,32},{1,33},{2,34},{3,35},{4,36},{5,37},{6,38},{7,39},{8,40},{9,... | collective-permute-start | bytes 2359304 | tf_op jit(solution)/shard_map/ppermute | solution.py:46
  126.6 8.4 %collective-permute-done.26.refs_6_ = bf16[4,32,2048]{2,1,0:T(8,128)(2,1)S(1)} collective-permute-done((bf16[4,32,2048]{2,1,0:T(8,128)(2,1)S(1)}, bf16[4,32,2048]{2,1,0:T(8,128)(2,1)S(1)}, u32[]{:S(2)}, u32[]{:S(2)}) %collective-permute-start.26) | collective-permute-done | bytes 524320 | tf_op jit(solution)/shard_map/ppermute | solution.py:25
  135.9 1.3 copy-done.5
  137.3 1.2 collective-permute-start.8
  138.5 8.1 %collective-permute-done.16.refs_5_ = bf16[4,4,16,1536]{3,2,1,0:T(8,128)(2,1)S(1)} collective-permute-done((bf16[4,4,16,1536]{3,2,1,0:T(8,128)(2,1)}, bf16[4,4,16,1536]{3,2,1,0:T(8,128)(2,1)S(1)}, u32[]{:S(2)}, u32[]{:S(2)}) %collective-permute-start.16) | collective-permute-done | bytes 786464 | tf_op jit(solution)/shard_map/ppermute | solution.py:46
  148.5 1.5 collective-permute-done.17.refs_6_
  150.9 3.6 %collective-permute-start.18 = (bf16[4,4,16,1536]{3,2,1,0:T(8,128)(2,1)}, bf16[4,4,16,1536]{3,2,1,0:T(8,128)(2,1)}, u32[]{:S(2)}, u32[]{:S(2)}) collective-permute-start(bf16[4,4,16,1536]{3,2,1,0:T(8,128)(2,1)} %pad_maximum_fusion.1.refs_4_), channel_id=1, source_target_pairs={{0,16},{1,17},{2,18},{3,19},{4,20},{5,21},{6,22},{7,23},{8,24},{9,... | collective-permute-start | bytes 2359304 | tf_op jit(solution)/shard_map/ppermute | solution.py:46
  154.6 1.6 copy-done.6
  156.2 1.0 copy-done.13
  157.3 1.0 copy-done.15
  158.3 1.0 copy-done.17
  159.3 1.0 copy-done.19
  160.4 1.0 copy-done.21
  161.4 1.0 copy-done.23
  162.5 8.6 %draft_logits.1 = (f32[1024,1024]{1,0:T(8,128)S(1)}, f32[8,1024]{1,0:T(8,128)S(1)}) custom-call(s32[16]{0:T(128)S(1)} %pad_add_fusion.place, bf16[4,32,2048]{2,1,0:T(8,128)(2,1)S(1)} %bitcast.94, bf16[4,32,2048]{2,1,0:T(8,128)(2,1)S(1)} %copy-done.15, bf16[4,32,2048]{2,1,0:T(8,128)(2,1)S(1)} %copy-done.17, ...), custom_call_target="tpu_custom_call" | custom-call | flops 4294967296 | bytes 12582912 | tf_op jit(solution)/shard_map/draft_logits/pallas_call | solution.py:177
  171.1 2.0 copy-done.2
  173.2 16.6 %teacher_logits.1 = (f32[1024,1024]{1,0:T(8,128)}, f32[8,1024]{1,0:T(8,128)S(1)}) custom-call(s32[16]{0:T(128)S(1)} %pad_add_fusion.place, bf16[4,4,16,2560]{3,2,1,0:T(8,128)(2,1)S(1)} %pad_maximum_fusion.refs_0_, bf16[4,4,16,2560]{3,2,1,0:T(8,128)(2,1)} %collective-permute-done.7.refs_1_, bf16[4,4,16,2560]{3,2,1,0:T(8,128)(2,1)} %collective-permute-done.8.refs_2_, ...), custom_call_target="tpu_custom_call" | custom-call | flops 8589934592 | bytes 20971520 | tf_op jit(solution)/shard_map/teacher_logits/pallas_call | solution.py:237
  190.5 4.5 %all-to-all-start.2 = ((f32[8,4,1024]{2,1,0:T(4,128)}), f32[8,4,1024]{2,1,0:T(4,128)S(1)}, u32[]{:S(2)}, u32[]{:S(2)}) async-start(f32[8,4,1024]{2,1,0:T(4,128)} %broadcast_in_dim.56), calls=%async_computation.2 | async-start | bytes 262144 | tf_op jit(solution)/shard_map/all_to_all | solution.py:452
  195.1 6.3 %all-to-all-done.2 = f32[8,4,1024]{2,1,0:T(4,128)S(1)} async-done(((f32[8,4,1024]{2,1,0:T(4,128)}), f32[8,4,1024]{2,1,0:T(4,128)S(1)}, u32[]{:S(2)}, u32[]{:S(2)}) %all-to-all-start.2) | async-done | bytes 131104 | tf_op jit(solution)/shard_map/all_to_all | solution.py:452
  202.5 13.6 %all-to-all-start.3 = ((f32[8,4,1024]{2,1,0:T(4,128)}), f32[8,4,1024]{2,1,0:T(4,128)S(1)}, u32[]{:S(2)}, u32[]{:S(2)}) async-start(f32[8,4,1024]{2,1,0:T(4,128)} %broadcast_in_dim.57), calls=%async_computation.3 | async-start | bytes 262144 | tf_op jit(solution)/shard_map/all_to_all | solution.py:452
  216.3 7.9 %all-to-all-done.3 = f32[8,4,1024]{2,1,0:T(4,128)S(1)} async-done(((f32[8,4,1024]{2,1,0:T(4,128)}), f32[8,4,1024]{2,1,0:T(4,128)S(1)}, u32[]{:S(2)}, u32[]{:S(2)}) %all-to-all-start.3) | async-done | bytes 131104 | tf_op jit(solution)/shard_map/all_to_all | solution.py:452
  224.7 2.2 copy-done.3
  226.9 1.6 copy-done.7
  228.5 8.8 %gradient_parts.1 = bf16[8,8,4,32,256]{4,3,2,1,0:T(8,128)(2,1)S(1)} custom-call(s32[2]{0:T(128)S(1)} %add_multiply_fusion.starts, f32[1024,1024]{1,0:T(8,128)S(1)} %copy-done.3, f32[1024,1024]{1,0:T(8,128)} %copy-done.2, f32[8,1024]{1,0:T(8,128)S(1)} %stack.106.rows_ref, bf16[512,2048]{1,0:T(8,128)(2,1)S(1)} %copy-done.4, bf16[512,2048]{1,0:T(8,128)(2,1)S(1)} %copy-done.7), custom_call_target="tpu_custom_call" | custom-call | flops 4294967296 | bytes 16777216 | tf_op jit(solution)/shard_map/gradient_parts/pallas_call | solution.py:286
  237.3 41.2 %all_to_all.25 = bf16[64,128,256]{2,1,0:T(8,128)(2,1)S(1)} all-to-all(bf16[64,128,256]{2,1,0:T(8,128)(2,1)S(1)} %bitcast.90), channel_id=1, replica_groups=mesh['yh'=2,'z'=4,'c'=2,'x'=4,'yl'=2] {'yh','z','x','yl'}, dimensions={0} | all-to-all | bytes 8388608 | tf_op jit(solution)/shard_map/all_to_all | solution.py:474
  278.5 1.3 convert_reduce_fusion
  (132 shorter events, 19.5 us)
Async XLA Ops:
  0.0 2.5 copy-start
  0.0 15.9 %copy-start.28 = (s32[32]{0:T(128)S(1)}, s32[32]{0:T(128)}, u32[]{:S(2)}) copy-start(s32[32]{0:T(128)} %param.25) | copy-start | bytes 388
  0.0 16.1 %copy-start.25 = (bf16[128,4096]{1,0:T(8,128)(2,1)S(1)}, bf16[128,4096]{1,0:T(8,128)(2,1)}, u32[]{:S(2)}) copy-start(bf16[128,4096]{1,0:T(8,128)(2,1)} %param.13) | copy-start | bytes 3145732
  0.0 16.1 %copy-start.29 = (f32[4096]{0:T(1024)S(1)}, f32[4096]{0:T(1024)}, u32[]{:S(2)}) copy-start(f32[4096]{0:T(1024)} %param.14) | copy-start | bytes 49156
  7.7 11.7 %copy-start.30 = (s32[4]{0:T(128)S(1)}, s32[4]{0:T(128)}, u32[]{:S(2)}) copy-start(s32[4]{0:T(128)} %param.24) | copy-start | bytes 52
  7.7 19.2 %all-to-all-start = ((bf16[8,128,256]{2,1,0:T(8,128)(2,1)}), bf16[8,128,256]{2,1,0:T(8,128)(2,1)S(1)}, u32[]{:S(2)}, u32[]{:S(2)}) async-start(bf16[8,128,256]{2,1,0:T(8,128)(2,1)} %broadcast_in_dim.46), calls=%async_computation | async-start | bytes 1048576 | tf_op jit(solution)/shard_map/all_to_all | solution.py:353
  26.9 1.9 collective-permute-start
  30.7 2.2 copy-start.24
  31.8 7.2 %copy-start.12 = (bf16[128,2048]{1,0:T(8,128)(2,1)S(1)}, bf16[128,2048]{1,0:T(8,128)(2,1)}, u32[]{:S(2)}) copy-start(bf16[128,2048]{1,0:T(8,128)(2,1)} %param.21) | copy-start | bytes 1572868
  32.9 25.3 %copy-start.26 = (f32[4096]{0:T(1024)S(1)}, f32[4096]{0:T(1024)}, u32[]{:S(2)}) copy-start(f32[4096]{0:T(1024)} %param.19) | copy-start | bytes 49156
  32.9 34.2 %copy-start.4 = (bf16[512,2048]{1,0:T(8,128)(2,1)S(1)}, bf16[512,2048]{1,0:T(8,128)(2,1)}, u32[]{:S(2)}) copy-start(bf16[512,2048]{1,0:T(8,128)(2,1)} %own_ref.1) | copy-start | bytes 6291460
  34.6 21.1 %all-to-all-start.1 = ((bf16[8,16,4096]{2,1,0:T(8,128)(2,1)}), bf16[8,16,4096]{2,1,0:T(8,128)(2,1)}, u32[]{:S(2)}, u32[]{:S(2)}) async-start(bf16[8,16,4096]{2,1,0:T(8,128)(2,1)} %bitcast.95), calls=%async_computation.1 | async-start | bytes 2097152 | tf_op jit(solution)/shard_map/all_to_all | solution.py:393
  39.1 20.5 %collective-permute-start.20 = (bf16[4,32,2048]{2,1,0:T(8,128)(2,1)S(1)}, bf16[4,32,2048]{2,1,0:T(8,128)(2,1)S(1)}, u32[]{:S(2)}, u32[]{:S(2)}) collective-permute-start(bf16[4,32,2048]{2,1,0:T(8,128)(2,1)S(1)} %bitcast.91), channel_id=1, source_target_pairs={{0,48},{16,0},{32,16},{48,32},{1,49},{17,1},{33,17},{49,33},{2,50}... | collective-permute-start | bytes 1572872 | tf_op jit(solution)/shard_map/ppermute | solution.py:25
  40.3 30.4 %collective-permute-start.22 = (bf16[4,32,2048]{2,1,0:T(8,128)(2,1)S(1)}, bf16[4,32,2048]{2,1,0:T(8,128)(2,1)}, u32[]{:S(2)}, u32[]{:S(2)}) collective-permute-start(bf16[4,32,2048]{2,1,0:T(8,128)(2,1)S(1)} %bitcast.92), channel_id=1, source_target_pairs={{0,16},{16,32},{32,48},{48,0},{1,17},{17,33},{33,49},{49,1},{2,18}... | collective-permute-start | bytes 1572872 | tf_op jit(solution)/shard_map/ppermute | solution.py:25
  41.2 23.9 %collective-permute-start.23 = (bf16[4,32,2048]{2,1,0:T(8,128)(2,1)S(1)}, bf16[4,32,2048]{2,1,0:T(8,128)(2,1)}, u32[]{:S(2)}, u32[]{:S(2)}) collective-permute-start(bf16[4,32,2048]{2,1,0:T(8,128)(2,1)S(1)} %bitcast.93), channel_id=1, source_target_pairs={{0,64},{64,0},{1,65},{65,1},{2,66},{66,2},{3,67},{67,3},{4,68},{68... | collective-permute-start | bytes 1572872 | tf_op jit(solution)/shard_map/ppermute | solution.py:25
  42.9 130.3 %collective-permute-start.19 = (bf16[512,4096]{1,0:T(8,128)(2,1)}, bf16[512,4096]{1,0:T(8,128)(2,1)}, u32[]{:S(2)}, u32[]{:S(2)}) collective-permute-start(bf16[512,4096]{1,0:T(8,128)(2,1)} %refs_8_.3), channel_id=1, source_target_pairs={{0,8},{8,0},{1,9},{9,1},{2,10},{10,2},{3,11},{11,3},{4,12},{12,4},... | collective-permute-start | bytes 12582920 | tf_op jit(solution)/shard_map/ppermute | solution.py:25
  59.2 7.9 %collective-permute-start.12 = (bf16[16,1536]{1,0:T(8,128)(2,1)S(1)}, bf16[16,1536]{1,0:T(8,128)(2,1)S(1)}, u32[]{:S(2)}, u32[]{:S(2)}) collective-permute-start(bf16[16,1536]{1,0:T(8,128)(2,1)S(1)} %get-tuple-element.24), channel_id=1, source_target_pairs={{0,2},{1,3},{2,4},{3,5},{4,6},{5,7},{6,0},{7,1},{8,9},{9,72},{10,1... | collective-permute-start | bytes 147464 | tf_op jit(solution)/shard_map/ppermute | solution.py:46
  59.6 66.8 %copy-start.14 = (bf16[4,32,2048]{2,1,0:T(8,128)(2,1)}, bf16[4,32,2048]{2,1,0:T(8,128)(2,1)S(1)}, u32[]{:S(2)}) copy-start(bf16[4,32,2048]{2,1,0:T(8,128)(2,1)S(1)} %collective-permute-done.20.refs_1_) | copy-start | bytes 1572868
  59.6 7.5 %collective-permute-start.11 = (bf16[16,1536]{1,0:T(8,128)(2,1)S(1)}, bf16[16,1536]{1,0:T(8,128)(2,1)S(1)}, u32[]{:S(2)}, u32[]{:S(2)}) collective-permute-start(bf16[16,1536]{1,0:T(8,128)(2,1)S(1)} %get-tuple-element.24), channel_id=1, source_target_pairs={{0,4},{1,5},{2,6},{3,7},{4,0},{5,1},{6,2},{7,3},{8,72},{9,73},{10,... | collective-permute-start | bytes 147464 | tf_op jit(solution)/shard_map/ppermute | solution.py:46
  65.1 4.1 %collective-permute-start.10 = (bf16[16,1536]{1,0:T(8,128)(2,1)S(1)}, bf16[16,1536]{1,0:T(8,128)(2,1)S(1)}, u32[]{:S(2)}, u32[]{:S(2)}) collective-permute-start(bf16[16,1536]{1,0:T(8,128)(2,1)S(1)} %get-tuple-element.24), channel_id=1, source_target_pairs={{0,6},{1,7},{2,0},{3,1},{4,2},{5,3},{6,4},{7,5},{8,73},{9,8},{10,7... | collective-permute-start | bytes 147464 | tf_op jit(solution)/shard_map/ppermute | solution.py:46
  67.1 68.9 %collective-permute-start.27 = (bf16[512,2048]{1,0:T(8,128)(2,1)S(1)}, bf16[512,2048]{1,0:T(8,128)(2,1)S(1)}, u32[]{:S(2)}, u32[]{:S(2)}) collective-permute-start(bf16[512,2048]{1,0:T(8,128)(2,1)S(1)} %copy-done.4), channel_id=1, source_target_pairs={{0,8},{8,0},{1,9},{9,1},{2,10},{10,2},{3,11},{11,3},{4,12},{12,4},... | collective-permute-start | bytes 6291464 | tf_op jit(solution)/shard_map/ppermute | solution.py:25
  67.1 14.9 %collective-permute-start.21 = (bf16[4,32,2048]{2,1,0:T(8,128)(2,1)S(1)}, bf16[4,32,2048]{2,1,0:T(8,128)(2,1)S(1)}, u32[]{:S(2)}, u32[]{:S(2)}) collective-permute-start(bf16[4,32,2048]{2,1,0:T(8,128)(2,1)S(1)} %collective-permute-done.20.refs_1_), channel_id=1, source_target_pairs={{0,48},{16,0},{32,16},{48,32},{1,49},{17,1},{33,17},{49,33},{2,50}... | collective-permute-start | bytes 1572872 | tf_op jit(solution)/shard_map/ppermute | solution.py:25
  69.2 23.5 %collective-permute-start.24 = (bf16[4,32,2048]{2,1,0:T(8,128)(2,1)}, bf16[4,32,2048]{2,1,0:T(8,128)(2,1)S(1)}, u32[]{:S(2)}, u32[]{:S(2)}) collective-permute-start(bf16[4,32,2048]{2,1,0:T(8,128)(2,1)} %collective-permute-done.23.refs_4_), channel_id=1, source_target_pairs={{0,48},{16,0},{32,16},{48,32},{1,49},{17,1},{33,17},{49,33},{2,50}... | collective-permute-start | bytes 1572872 | tf_op jit(solution)/shard_map/ppermute | solution.py:25
  70.7 31.4 %collective-permute-start.15 = (bf16[4,16,1536]{2,1,0:T(8,128)(2,1)S(1)}, bf16[4,16,1536]{2,1,0:T(8,128)(2,1)S(1)}, u32[]{:S(2)}, u32[]{:S(2)}) collective-permute-start(bf16[4,16,1536]{2,1,0:T(8,128)(2,1)S(1)} %get-tuple-element.22), channel_id=1, source_target_pairs={{0,1},{1,64},{2,3},{3,66},{4,5},{5,68},{6,7},{7,70},{8,10},{9,11},... | collective-permute-start | bytes 589832 | tf_op jit(solution)/shard_map/ppermute | solution.py:46
  82.0 0.8 copy-start.16
  82.8 11.8 %collective-permute-start.3 = (bf16[16,2560]{1,0:T(8,128)(2,1)S(1)}, bf16[16,2560]{1,0:T(8,128)(2,1)S(1)}, u32[]{:S(2)}, u32[]{:S(2)}) collective-permute-start(bf16[16,2560]{1,0:T(8,128)(2,1)S(1)} %get-tuple-element.26), channel_id=1, source_target_pairs={{0,16},{1,17},{2,18},{3,19},{4,20},{5,21},{6,22},{7,23},{8,24},{9,... | collective-permute-start | bytes 245768 | tf_op jit(solution)/shard_map/ppermute | solution.py:46
  92.7 0.8 copy-start.18
  93.4 5.9 %collective-permute-start.2 = (bf16[16,2560]{1,0:T(8,128)(2,1)S(1)}, bf16[16,2560]{1,0:T(8,128)(2,1)S(1)}, u32[]{:S(2)}, u32[]{:S(2)}) collective-permute-start(bf16[16,2560]{1,0:T(8,128)(2,1)S(1)} %get-tuple-element.26), channel_id=1, source_target_pairs={{0,32},{1,33},{2,34},{3,35},{4,36},{5,37},{6,38},{7,39},{8,40},{9,... | collective-permute-start | bytes 245768 | tf_op jit(solution)/shard_map/ppermute | solution.py:46
  94.6 6.0 %collective-permute-start.1 = (bf16[16,2560]{1,0:T(8,128)(2,1)S(1)}, bf16[16,2560]{1,0:T(8,128)(2,1)S(1)}, u32[]{:S(2)}, u32[]{:S(2)}) collective-permute-start(bf16[16,2560]{1,0:T(8,128)(2,1)S(1)} %get-tuple-element.26), channel_id=1, source_target_pairs={{0,48},{1,49},{2,50},{3,51},{4,52},{5,53},{6,54},{7,55},{8,56},{9,... | collective-permute-start | bytes 245768 | tf_op jit(solution)/shard_map/ppermute | solution.py:46
  99.4 13.8 %collective-permute-start.25 = (bf16[4,32,2048]{2,1,0:T(8,128)(2,1)}, bf16[4,32,2048]{2,1,0:T(8,128)(2,1)S(1)}, u32[]{:S(2)}, u32[]{:S(2)}) collective-permute-start(bf16[4,32,2048]{2,1,0:T(8,128)(2,1)} %collective-permute-done.23.refs_4_), channel_id=1, source_target_pairs={{0,16},{16,32},{32,48},{48,0},{1,17},{17,33},{33,49},{49,1},{2,18}... | collective-permute-start | bytes 1572872 | tf_op jit(solution)/shard_map/ppermute | solution.py:25
  100.6 7.2 %collective-permute-start.14 = (bf16[4,16,1536]{2,1,0:T(8,128)(2,1)S(1)}, bf16[4,16,1536]{2,1,0:T(8,128)(2,1)S(1)}, u32[]{:S(2)}, u32[]{:S(2)}) collective-permute-start(bf16[4,16,1536]{2,1,0:T(8,128)(2,1)S(1)} %get-tuple-element.22), channel_id=1, source_target_pairs={{0,64},{1,65},{2,66},{3,67},{4,68},{5,69},{6,70},{7,71},{8,12},{9,... | collective-permute-start | bytes 589832 | tf_op jit(solution)/shard_map/ppermute | solution.py:46
  102.1 7.9 %collective-permute-start.13 = (bf16[4,16,1536]{2,1,0:T(8,128)(2,1)S(1)}, bf16[4,16,1536]{2,1,0:T(8,128)(2,1)S(1)}, u32[]{:S(2)}, u32[]{:S(2)}) collective-permute-start(bf16[4,16,1536]{2,1,0:T(8,128)(2,1)S(1)} %get-tuple-element.22), channel_id=1, source_target_pairs={{0,65},{1,0},{2,67},{3,2},{4,69},{5,4},{6,71},{7,6},{8,14},{9,15},... | collective-permute-start | bytes 589832 | tf_op jit(solution)/shard_map/ppermute | solution.py:46
  107.8 8.3 %collective-permute-start.6 = (bf16[4,16,2560]{2,1,0:T(8,128)(2,1)S(1)}, bf16[4,16,2560]{2,1,0:T(8,128)(2,1)S(1)}, u32[]{:S(2)}, u32[]{:S(2)}) collective-permute-start(bf16[4,16,2560]{2,1,0:T(8,128)(2,1)S(1)} %get-tuple-element.18), channel_id=1, source_target_pairs={{0,1},{1,64},{2,3},{3,66},{4,5},{5,68},{6,7},{7,70},{8,10},{9,11},... | collective-permute-start | bytes 983048 | tf_op jit(solution)/shard_map/ppermute | solution.py:46
  110.0 10.7 %collective-permute-start.5 = (bf16[4,16,2560]{2,1,0:T(8,128)(2,1)S(1)}, bf16[4,16,2560]{2,1,0:T(8,128)(2,1)S(1)}, u32[]{:S(2)}, u32[]{:S(2)}) collective-permute-start(bf16[4,16,2560]{2,1,0:T(8,128)(2,1)S(1)} %get-tuple-element.18), channel_id=1, source_target_pairs={{0,64},{1,65},{2,66},{3,67},{4,68},{5,69},{6,70},{7,71},{8,12},{9,... | collective-permute-start | bytes 983048 | tf_op jit(solution)/shard_map/ppermute | solution.py:46
  113.1 36.9 %copy-start.20 = (bf16[4,32,2048]{2,1,0:T(8,128)(2,1)}, bf16[4,32,2048]{2,1,0:T(8,128)(2,1)S(1)}, u32[]{:S(2)}) copy-start(bf16[4,32,2048]{2,1,0:T(8,128)(2,1)S(1)} %collective-permute-done.25.refs_7_) | copy-start | bytes 1572868
  113.1 33.4 %collective-permute-start.16 = (bf16[4,4,16,1536]{3,2,1,0:T(8,128)(2,1)}, bf16[4,4,16,1536]{3,2,1,0:T(8,128)(2,1)S(1)}, u32[]{:S(2)}, u32[]{:S(2)}) collective-permute-start(bf16[4,4,16,1536]{3,2,1,0:T(8,128)(2,1)} %pad_maximum_fusion.1.refs_4_), channel_id=1, source_target_pairs={{0,48},{1,49},{2,50},{3,51},{4,52},{5,53},{6,54},{7,55},{8,56},{9,... | collective-permute-start | bytes 2359304 | tf_op jit(solution)/shard_map/ppermute | solution.py:46
  116.1 7.1 %collective-permute-start.4 = (bf16[4,16,2560]{2,1,0:T(8,128)(2,1)S(1)}, bf16[4,16,2560]{2,1,0:T(8,128)(2,1)S(1)}, u32[]{:S(2)}, u32[]{:S(2)}) collective-permute-start(bf16[4,16,2560]{2,1,0:T(8,128)(2,1)S(1)} %get-tuple-element.18), channel_id=1, source_target_pairs={{0,65},{1,0},{2,67},{3,2},{4,69},{5,4},{6,71},{7,6},{8,14},{9,15},... | collective-permute-start | bytes 983048 | tf_op jit(solution)/shard_map/ppermute | solution.py:46
  120.7 14.3 %collective-permute-start.26 = (bf16[4,32,2048]{2,1,0:T(8,128)(2,1)S(1)}, bf16[4,32,2048]{2,1,0:T(8,128)(2,1)S(1)}, u32[]{:S(2)}, u32[]{:S(2)}) collective-permute-start(bf16[4,32,2048]{2,1,0:T(8,128)(2,1)S(1)} %collective-permute-done.25.refs_7_), channel_id=1, source_target_pairs={{0,16},{16,32},{32,48},{48,0},{1,17},{17,33},{33,49},{49,1},{2,18}... | collective-permute-start | bytes 1572872 | tf_op jit(solution)/shard_map/ppermute | solution.py:25
  123.2 26.8 %collective-permute-start.17 = (bf16[4,4,16,1536]{3,2,1,0:T(8,128)(2,1)}, bf16[4,4,16,1536]{3,2,1,0:T(8,128)(2,1)S(1)}, u32[]{:S(2)}, u32[]{:S(2)}) collective-permute-start(bf16[4,4,16,1536]{3,2,1,0:T(8,128)(2,1)} %pad_maximum_fusion.1.refs_4_), channel_id=1, source_target_pairs={{0,32},{1,33},{2,34},{3,35},{4,36},{5,37},{6,38},{7,39},{8,40},{9,... | collective-permute-start | bytes 2359304 | tf_op jit(solution)/shard_map/ppermute | solution.py:46
  135.0 0.8 copy-start.22
  135.9 37.3 %collective-permute-start.7 = (bf16[4,4,16,2560]{3,2,1,0:T(8,128)(2,1)S(1)}, bf16[4,4,16,2560]{3,2,1,0:T(8,128)(2,1)}, u32[]{:S(2)}, u32[]{:S(2)}) collective-permute-start(bf16[4,4,16,2560]{3,2,1,0:T(8,128)(2,1)S(1)} %pad_maximum_fusion.refs_0_), channel_id=1, source_target_pairs={{0,6},{1,7},{2,0},{3,1},{4,2},{5,3},{6,4},{7,5},{8,73},{9,8},{10,7... | collective-permute-start | bytes 3932168 | tf_op jit(solution)/shard_map/ppermute | solution.py:46
  135.9 1.3 copy-start.5
  137.3 35.9 %collective-permute-start.8 = (bf16[4,4,16,2560]{3,2,1,0:T(8,128)(2,1)S(1)}, bf16[4,4,16,2560]{3,2,1,0:T(8,128)(2,1)}, u32[]{:S(2)}, u32[]{:S(2)}) collective-permute-start(bf16[4,4,16,2560]{3,2,1,0:T(8,128)(2,1)S(1)} %pad_maximum_fusion.refs_0_), channel_id=1, source_target_pairs={{0,4},{1,5},{2,6},{3,7},{4,0},{5,1},{6,2},{7,3},{8,72},{9,73},{10,... | collective-permute-start | bytes 3932168 | tf_op jit(solution)/shard_map/ppermute | solution.py:46
  146.6 0.9 copy-start.8
  147.5 25.6 %collective-permute-start.9 = (bf16[4,4,16,2560]{3,2,1,0:T(8,128)(2,1)S(1)}, bf16[4,4,16,2560]{3,2,1,0:T(8,128)(2,1)}, u32[]{:S(2)}, u32[]{:S(2)}) collective-permute-start(bf16[4,4,16,2560]{3,2,1,0:T(8,128)(2,1)S(1)} %pad_maximum_fusion.refs_0_), channel_id=1, source_target_pairs={{0,2},{1,3},{2,4},{3,5},{4,6},{5,7},{6,0},{7,1},{8,9},{9,72},{10,1... | collective-permute-start | bytes 3932168 | tf_op jit(solution)/shard_map/ppermute | solution.py:46
  150.0 0.9 copy-start.10
  150.9 22.2 %collective-permute-start.18 = (bf16[4,4,16,1536]{3,2,1,0:T(8,128)(2,1)}, bf16[4,4,16,1536]{3,2,1,0:T(8,128)(2,1)}, u32[]{:S(2)}, u32[]{:S(2)}) collective-permute-start(bf16[4,4,16,1536]{3,2,1,0:T(8,128)(2,1)} %pad_maximum_fusion.1.refs_4_), channel_id=1, source_target_pairs={{0,16},{1,17},{2,18},{3,19},{4,20},{5,21},{6,22},{7,23},{8,24},{9,... | collective-permute-start | bytes 2359304 | tf_op jit(solution)/shard_map/ppermute | solution.py:46
  154.6 1.6 copy-start.6
  156.2 1.0 copy-start.13
  157.3 1.0 copy-start.15
  158.3 1.0 copy-start.17
  159.3 1.0 copy-start.19
  160.4 1.0 copy-start.21
  161.4 1.0 copy-start.23
  162.5 10.7 %copy-start.9 = (bf16[4,4,16,1536]{3,2,1,0:T(8,128)(2,1)S(1)}, bf16[4,4,16,1536]{3,2,1,0:T(8,128)(2,1)}, u32[]{:S(2)}) copy-start(bf16[4,4,16,1536]{3,2,1,0:T(8,128)(2,1)} %copy-done.8) | copy-start | bytes 2359300
  162.5 10.7 %copy-start.11 = (bf16[4,4,16,1536]{3,2,1,0:T(8,128)(2,1)S(1)}, bf16[4,4,16,1536]{3,2,1,0:T(8,128)(2,1)}, u32[]{:S(2)}) copy-start(bf16[4,4,16,1536]{3,2,1,0:T(8,128)(2,1)} %copy-done.10) | copy-start | bytes 2359300
  171.1 2.0 copy-start.2
  173.2 21.8 %copy-start.27 = (s32[2048]{0:T(1024)S(1)}, s32[2048]{0:T(1024)}, u32[]{:S(2)}) copy-start(s32[2048]{0:T(1024)} %param.23) | copy-start | bytes 24580
  190.5 10.9 %all-to-all-start.2 = ((f32[8,4,1024]{2,1,0:T(4,128)}), f32[8,4,1024]{2,1,0:T(4,128)S(1)}, u32[]{:S(2)}, u32[]{:S(2)}) async-start(f32[8,4,1024]{2,1,0:T(4,128)} %broadcast_in_dim.56), calls=%async_computation.2 | async-start | bytes 262144 | tf_op jit(solution)/shard_map/all_to_all | solution.py:452
  202.5 21.6 %all-to-all-start.3 = ((f32[8,4,1024]{2,1,0:T(4,128)}), f32[8,4,1024]{2,1,0:T(4,128)S(1)}, u32[]{:S(2)}, u32[]{:S(2)}) async-start(f32[8,4,1024]{2,1,0:T(4,128)} %broadcast_in_dim.57), calls=%async_computation.3 | async-start | bytes 262144 | tf_op jit(solution)/shard_map/all_to_all | solution.py:452
  224.7 2.2 copy-start.3
  226.9 1.6 copy-start.7
  237.3 42.5 %copy-start.1 = (bf16[4096,128]{1,0:T(8,128)(2,1)S(1)}, bf16[4096,128]{1,0:T(8,128)(2,1)}, u32[]{:S(2)}) copy-start(bf16[4096,128]{1,0:T(8,128)(2,1)} %param.17) | copy-start | bytes 3145732

commit v2 on v1

--- a/solution.py
+++ b/solution.py
@@ -15,7 +15,7 @@
 
 CTX = ("yh", "z", "c")
 VOCAB = ("x", "yl")
-Z, C = ("z",), ("c",)
+X, Y, Z, C = ("x",), ("yh", "yl"), ("z",), ("c",)
 CHIPS = ("yh", "z", "x", "yl")
 F32, BF16 = jnp.float32, jnp.bfloat16
 
@@ -224,7 +224,7 @@
     @pl.when(pl.program_id(0) == pl.num_programs(0) - 1)
     def _():
         teacher = totals_rows(top_ref, sum_ref)
-        stats_ref[...] = jnp.concatenate([teacher[0:2], draft_stats[0:2], teacher[4:8]], axis=0)
+        stats_ref[...] = jnp.concatenate([teacher[0:2], draft_stats[0:2]], axis=0)
 
 
 def teacher_logits(place, parts, own, other, draft_stats):
@@ -242,13 +242,13 @@
             in_specs=whole + [HELD, HELD, pl.BlockSpec((8, count), lambda j, s: (0, 0))],
             out_specs=[
                 pl.BlockSpec((count, BLOCK), lambda j, s: (0, j)),
-                pl.BlockSpec((8, count), lambda j, s: (0, 0)),
+                pl.BlockSpec((4, count), lambda j, s: (0, 0)),
             ],
             scratch_shapes=logits_scratch(count, width),
         ),
         out_shape=[
             jax.ShapeDtypeStruct((count, words), F32),
-            jax.ShapeDtypeStruct((8, count), F32),
+            jax.ShapeDtypeStruct((4, count), F32),
         ],
         compiler_params=pltpu.CompilerParams(vmem_limit_bytes=48 << 20),
         cost_estimate=pl.CostEstimate(
@@ -305,6 +305,51 @@
         ),
         name="gradient_parts",
     )(starts, teacher, draft, rows, own, other)
+
+
+def keys_kernel(hidden_from, key_from, value_from, gain_ref, cosine_ref, sine_ref, *refs):
+    normed_ref, copies_ref, hidden_ref, key_ref, value_ref, arrived = refs
+    fetches = [
+        pltpu.make_async_copy(hidden_from, hidden_ref, arrived.at[0]),
+        pltpu.make_async_copy(key_from, key_ref, arrived.at[1]),
+        pltpu.make_async_copy(value_from, value_ref, arrived.at[2]),
+    ]
+    for fetch in fetches:
+        fetch.start()
+    fetches[0].wait()
+    values = hidden_ref[...].astype(F32)
+    mean_square = jnp.mean(values * values, axis=-1, keepdims=True)
+    normed = (values * lax.rsqrt(mean_square + EPSILON) * gain_ref[...]).astype(BF16)
+    normed_ref[...] = normed
+    fetches[1].wait()
+    keys = jnp.dot(normed, key_ref[...], preferred_element_type=F32)
+    turned = keys * cosine_ref[...] + pltpu.roll(keys, HEAD_DIM // 2, 1) * sine_ref[...]
+    fetches[2].wait()
+    passed = jnp.dot(normed, value_ref[...], preferred_element_type=F32)
+    both = jnp.concatenate([turned.astype(BF16), passed.astype(BF16)], axis=1)
+    for k in range(copies_ref.shape[0]):
+        copies_ref[k] = both
+
+
+def keys_and_values(hidden, gain, w_key, w_value, cosine, sine, copies):
+    rows, width = hidden.shape
+    large = [pltpu.with_memory_space_constraint(a, pltpu.HBM) for a in (hidden, w_key, w_value)]
+    whole = pl.BlockSpec(memory_space=pltpu.VMEM)
+    return pl.pallas_call(
+        keys_kernel,
+        in_specs=[HELD] * 3 + [whole] * 3,
+        out_shape=[
+            jax.ShapeDtypeStruct((rows, width), BF16),
+            jax.ShapeDtypeStruct((copies, rows, 2 * HEAD_DIM), BF16),
+        ],
+        scratch_shapes=[pltpu.VMEM(a.shape, BF16) for a in large]
+        + [pltpu.SemaphoreType.DMA((3,))],
+        compiler_params=pltpu.CompilerParams(vmem_limit_bytes=24 << 20),
+        cost_estimate=pl.CostEstimate(
+            flops=4 * rows * width * HEAD_DIM, transcendentals=rows, bytes_accessed=5 << 20
+        ),
+        name="keys_and_values",
+    )(*large, gain[None, :], cosine, sine)
 
 
 def on_device(
@@ -342,14 +387,18 @@
 
     lines = jnp.arange(row_count, dtype=jnp.int32)
     query_pos, query_roll = locate(lax.axis_index(CTX) * row_count + lines)
-    normed = rms_scale(hidden_in.astype(F32), attn_gain).astype(BF16)
-    keys = jnp.dot(normed, w_key, preferred_element_type=F32).reshape(
-        row_count, local_groups, head_dim
-    )
-    keys = rotate(keys, query_pos).astype(BF16).reshape(row_count, local_groups * head_dim)
-    values = jnp.dot(normed, w_value, preferred_element_type=F32).astype(BF16)
-    both = jnp.concatenate([keys, values], axis=1)
-    copies = jnp.broadcast_to(both[None], (8, *both.shape))
+    exponents = jnp.arange(head_dim // 2, dtype=F32) * (2.0 / head_dim)
+    angles = query_pos.astype(F32)[:, None] * jnp.power(ROPE_BASE, -exponents)[None, :]
+    cosine, sine = jnp.cos(angles), jnp.sin(angles)
+    normed, copies = keys_and_values(
+        hidden_in,
+        attn_gain,
+        w_key,
+        w_value,
+        jnp.concatenate([cosine, cosine], axis=1),
+        jnp.concatenate([-sine, sine], axis=1),
+        8,
+    )
     both = lax.all_to_all(copies, ("yh", "z"), split_axis=0, concat_axis=0, tiled=True)
     both = both.reshape(8 * row_count, -1)
     both = ring(both, C)
@@ -447,9 +496,8 @@
         sums = jnp.sum(pieces[:, 1::2] * jnp.exp(pieces[:, 0::2] - tops), axis=0)
         return jnp.stack([tops[0], sums[0], tops[1], sums[1]])
 
-    for axes in (("x", "yl"), ("yh", "z")):
-        copies = jnp.broadcast_to(stats[None, :4], (8, *stats[:4].shape))
-        stats = merged(lax.all_to_all(copies, axes, split_axis=0, concat_axis=0, tiled=True))
+    for axes in (X, Y, Z):
+        stats = merged(jnp.stack(ring(stats, axes)))
     targets = target_ids.reshape(2, 4, 2, 4, 2 * share_rows)
     targets = lax.dynamic_index_in_dim(targets, my_c, 2, keepdims=False)
     targets = jnp.transpose(targets, (2, 0, 1, 3)).reshape(-1).astype(F32)

time: 281 us -> 278 us (0.989)
  waiting for transfers between devices: 86.2 us -> 77.7 us
  starting transfers between devices: 71.1 us -> 77.1 us
  matrix products: 10.6 us -> 6.59 us
  blocking collectives: 41.2 us -> 44.9 us
  Pallas kernels: 34.1 us -> 37.7 us
    ppermute x10 -> x19, starting transfers between devices: 8.9 us -> 33.1 us  [shifted(): return lax.ppermute(a, axes, [(i, (i + k) % n) for i in range(n)])]
    all_to_all x2 -> x0, starting transfers between devices: 18 us -> none  [on_device(): lax.all_to_all(copies, axes, split_axis=0, concat_axis=0, tiled=True)]
    all_to_all x2 -> x0, waiting for transfers between devices: 14.2 us -> none  [on_device(): lax.all_to_all(copies, axes, split_axis=0, concat_axis=0, tiled=True)]
    ppermute x10 -> x19, waiting for transfers between devices: 31.3 us -> 36.7 us  [shifted(): return lax.ppermute(a, axes, [(i, (i + k) % n) for i in range(n)])]
    dot_general x2 -> x0, matrix products: 4.02 us -> none  [the longest x1 2.17 us: on_device(): jnp.dot(normed, w_key, preferred_element_type=F32)]
    all_to_all x1, blocking collectives: 41.2 us -> 44.9 us  [on_device(): lax.all_to_all(parts, CHIPS, split_axis=0, concat_axis=0, tiled=True)]
    pallas_call x0 -> x1, Pallas kernels: none -> 3.65 us  [keys_and_values(): pl.pallas_call(keys_kernel, in_specs=[HELD] * 3 + [whole] * 3, out_shape=...]
    unnamed x62 -> x56, local copies, waits for them, and re-layouts: 20.3 us -> 21 us
  transfers between devices with their start and end apart: 32 -> 39, of which waited for: 18 -> 22; matrix products, arithmetic and copies ran while one was open for 4% -> 4% of each run, Pallas kernels for 3% -> 3%
where the time goes in v2:
time: 278 us; the launch traced here: 277 us
  waiting for transfers between devices  77.7 us (28%)
  starting transfers between devices  77.1 us (28%)
  blocking collectives  44.9 us (16%)
  Pallas kernels  37.7 us (14%)
  local copies, waits for them, and re-layouts  21.9 us (8%)
  other arithmetic  10.6 us (4%)
  matrix products  6.59 us (2%)
    all_to_all x1, blocking collectives, on_device(): lax.all_to_all(parts, CHIPS, split_axis=0, concat_axis=0, tiled=True)  44.9 us
    ppermute x19, waiting for transfers between devices, shifted(): return lax.ppermute(a, axes, [(i, (i + k) % n) for i in range(n)])  36.7 us
    ppermute x19, starting transfers between devices, shifted(): return lax.ppermute(a, axes, [(i, (i + k) % n) for i in range(n)])  33.1 us
    ppermute x18, starting transfers between devices, moved(): return lax.ppermute(a, EVERY, pairs)  31.6 us
    unnamed x56, local copies, waits for them, and re-layouts  21 us
    ppermute x18, waiting for transfers between devices, moved(): return lax.ppermute(a, EVERY, pairs)  21 us
    pallas_call x1, Pallas kernels, teacher_logits(): pl.pallas_call(teacher_kernel, grid_spec=pltpu.PrefetchScalarGridSpec(num...  16.7 us
    all_to_all x1, waiting for transfers between devices, on_device(): lax.all_to_all(partial_value.reshape(shares, share_rows, -1), VOCAB, spli...  12.8 us
  transfers between devices with their start and end apart: 39, of which 22 were waited for; matrix products, arithmetic and copies ran while one was open for 4% of the time, Pallas kernels for 3%

profile of v2, /device:TPU:0, one launch (start us, length us, event | category | flops | bytes accessed | tf_op | source)
XLA Modules:
  0.0 277.1 jit_solution(17493537427450668515)
XLA Ops:
  2.0 3.7 %keys_and_values.1 = (bf16[128,4096]{1,0:T(8,128)(2,1)S(1)}, bf16[8,128,256]{2,1,0:T(8,128)(2,1)}) custom-call(bf16[128,4096]{1,0:T(8,128)(2,1)} %hidden_from.1, bf16[4096,128]{1,0:T(8,128)(2,1)} %key_from.1, bf16[4096,128]{1,0:T(8,128)(2,1)} %value_from.1, f32[1,4096]{1,0:T(1,128)S(1)} %bitcast.99, f32[128,128]{1,0:T(8,128)S(1)} %get-tuple-element.56.cosine_ref, ...), custom_call_target="tpu_custom_call" | custom-call | flops 268435456 | bytes 5242880 | tf_op jit(solution)/shard_map/keys_and_values/pallas_call | solution.py:338
  5.7 8.1 %all-to-all-start = ((bf16[8,128,256]{2,1,0:T(8,128)(2,1)}), bf16[8,128,256]{2,1,0:T(8,128)(2,1)S(1)}, u32[]{:S(2)}, u32[]{:S(2)}) async-start(bf16[8,128,256]{2,1,0:T(8,128)(2,1)} %get-tuple-element.11), calls=%async_computation | async-start | bytes 1048576 | tf_op jit(solution)/shard_map/all_to_all | solution.py:402
  13.9 2.9 %fusion.75 = f32[128,512]{1,0:T(8,128)S(1)} fusion(bf16[128,4096]{1,0:T(8,128)(2,1)S(1)} %get-tuple-element.12, bf16[4096,512]{1,0:T(8,128)(2,1)} %param.15), kind=kOutput, calls=%fused_computation.153 | convolution fusion | flops 536870912 | bytes 5505024 | tf_op jit(solution)/shard_map/dot_general | solution.py:410
  17.5 7.3 %all-to-all-done = bf16[8,128,256]{2,1,0:T(8,128)(2,1)S(1)} async-done(((bf16[8,128,256]{2,1,0:T(8,128)(2,1)}), bf16[8,128,256]{2,1,0:T(8,128)(2,1)S(1)}, u32[]{:S(2)}, u32[]{:S(2)}) %all-to-all-start) | async-done | bytes 524320 | tf_op jit(solution)/shard_map/all_to_all | solution.py:402
  24.8 1.3 compare_and_fusion
  27.5 1.0 fusion.1
  28.5 1.1 fusion.13
  30.7 1.7 convolution_convert_fusion
  32.5 4.4 %all-to-all-start.1 = ((bf16[8,16,4096]{2,1,0:T(8,128)(2,1)}), bf16[8,16,4096]{2,1,0:T(8,128)(2,1)}, u32[]{:S(2)}, u32[]{:S(2)}) async-start(bf16[8,16,4096]{2,1,0:T(8,128)(2,1)} %bitcast.105), calls=%async_computation.1 | async-start | bytes 2097152 | tf_op jit(solution)/shard_map/all_to_all | solution.py:442
  36.9 1.2 collective-permute-start.20
  39.0 1.7 collective-permute-start.23
  40.7 12.8 %all-to-all-done.1 = bf16[8,16,4096]{2,1,0:T(8,128)(2,1)} async-done(((bf16[8,16,4096]{2,1,0:T(8,128)(2,1)}), bf16[8,16,4096]{2,1,0:T(8,128)(2,1)}, u32[]{:S(2)}, u32[]{:S(2)}) %all-to-all-start.1) | async-done | bytes 1048608 | tf_op jit(solution)/shard_map/all_to_all | solution.py:442
  53.5 1.4 convert_reduce_fusion.1
  54.9 1.1 multiply_reduce_fusion
  57.4 2.2 collective-permute-start.11
  59.6 3.3 %collective-permute-done.23.refs_4_ = bf16[4,32,2048]{2,1,0:T(8,128)(2,1)} collective-permute-done((bf16[4,32,2048]{2,1,0:T(8,128)(2,1)S(1)}, bf16[4,32,2048]{2,1,0:T(8,128)(2,1)}, u32[]{:S(2)}, u32[]{:S(2)}) %collective-permute-start.23) | collective-permute-done | bytes 524320 | tf_op jit(solution)/shard_map/ppermute | solution.py:25
  62.9 2.0 collective-permute-start.10
  64.9 1.5 collective-permute-start.21
  67.0 1.5 collective-permute-start.24
  68.5 1.2 collective-permute-start.15
  69.8 10.0 %collective-permute-done.21.refs_2_ = bf16[4,32,2048]{2,1,0:T(8,128)(2,1)S(1)} collective-permute-done((bf16[4,32,2048]{2,1,0:T(8,128)(2,1)S(1)}, bf16[4,32,2048]{2,1,0:T(8,128)(2,1)S(1)}, u32[]{:S(2)}, u32[]{:S(2)}) %collective-permute-start.21) | collective-permute-done | bytes 524320 | tf_op jit(solution)/shard_map/ppermute | solution.py:25
  81.5 9.0 %collective-permute-done.24.refs_5_ = bf16[4,32,2048]{2,1,0:T(8,128)(2,1)S(1)} collective-permute-done((bf16[4,32,2048]{2,1,0:T(8,128)(2,1)}, bf16[4,32,2048]{2,1,0:T(8,128)(2,1)S(1)}, u32[]{:S(2)}, u32[]{:S(2)}) %collective-permute-start.24) | collective-permute-done | bytes 524320 | tf_op jit(solution)/shard_map/ppermute | solution.py:25
  91.3 1.2 collective-permute-start.2
  92.5 2.4 collective-permute-start.1
  94.8 2.4 collective-permute-done.2
  97.2 1.2 collective-permute-start.25
  98.5 1.5 collective-permute-start.14
  100.0 2.7 collective-permute-start.13
  102.7 2.9 %collective-permute-done.14 = bf16[4,16,1536]{2,1,0:T(8,128)(2,1)S(1)} collective-permute-done((bf16[4,16,1536]{2,1,0:T(8,128)(2,1)S(1)}, bf16[4,16,1536]{2,1,0:T(8,128)(2,1)S(1)}, u32[]{:S(2)}, u32[]{:S(2)}) %collective-permute-start.14) | collective-permute-done | bytes 196640 | tf_op jit(solution)/shard_map/ppermute | solution.py:46
  105.6 1.6 collective-permute-start.6
  107.9 2.1 collective-permute-start.5
  111.0 2.6 collective-permute-start.16
  113.9 1.7 collective-permute-start.4
  115.6 2.9 %collective-permute-done.5 = bf16[4,16,2560]{2,1,0:T(8,128)(2,1)S(1)} collective-permute-done((bf16[4,16,2560]{2,1,0:T(8,128)(2,1)S(1)}, bf16[4,16,2560]{2,1,0:T(8,128)(2,1)S(1)}, u32[]{:S(2)}, u32[]{:S(2)}) %collective-permute-start.5) | collective-permute-done | bytes 327712 | tf_op jit(solution)/shard_map/ppermute | solution.py:46
  119.4 1.6 collective-permute-done.4
  121.0 3.3 %collective-permute-start.17 = (bf16[4,4,16,1536]{3,2,1,0:T(8,128)(2,1)}, bf16[4,4,16,1536]{3,2,1,0:T(8,128)(2,1)S(1)}, u32[]{:S(2)}, u32[]{:S(2)}) collective-permute-start(bf16[4,4,16,1536]{3,2,1,0:T(8,128)(2,1)} %pad_maximum_fusion.1.refs_4_), channel_id=1, source_target_pairs={{0,32},{1,33},{2,34},{3,35},{4,36},{5,37},{6,38},{7,39},{8,40},{9,... | collective-permute-start | bytes 2359304 | tf_op jit(solution)/shard_map/ppermute | solution.py:46
  124.4 8.4 %collective-permute-done.26.refs_6_ = bf16[4,32,2048]{2,1,0:T(8,128)(2,1)S(1)} collective-permute-done((bf16[4,32,2048]{2,1,0:T(8,128)(2,1)S(1)}, bf16[4,32,2048]{2,1,0:T(8,128)(2,1)S(1)}, u32[]{:S(2)}, u32[]{:S(2)}) %collective-permute-start.26) | collective-permute-done | bytes 524320 | tf_op jit(solution)/shard_map/ppermute | solution.py:25
  133.8 1.3 copy-done.3
  135.1 1.2 collective-permute-start.8
  136.3 8.1 %collective-permute-done.16.refs_5_ = bf16[4,4,16,1536]{3,2,1,0:T(8,128)(2,1)S(1)} collective-permute-done((bf16[4,4,16,1536]{3,2,1,0:T(8,128)(2,1)}, bf16[4,4,16,1536]{3,2,1,0:T(8,128)(2,1)S(1)}, u32[]{:S(2)}, u32[]{:S(2)}) %collective-permute-start.16) | collective-permute-done | bytes 786464 | tf_op jit(solution)/shard_map/ppermute | solution.py:46
  146.4 1.5 collective-permute-done.17.refs_6_
  148.7 3.6 %collective-permute-start.18 = (bf16[4,4,16,1536]{3,2,1,0:T(8,128)(2,1)}, bf16[4,4,16,1536]{3,2,1,0:T(8,128)(2,1)}, u32[]{:S(2)}, u32[]{:S(2)}) collective-permute-start(bf16[4,4,16,1536]{3,2,1,0:T(8,128)(2,1)} %pad_maximum_fusion.1.refs_4_), channel_id=1, source_target_pairs={{0,16},{1,17},{2,18},{3,19},{4,20},{5,21},{6,22},{7,23},{8,24},{9,... | collective-permute-start | bytes 2359304 | tf_op jit(solution)/shard_map/ppermute | solution.py:46
  152.5 1.6 copy-done.4
  155.1 1.0 copy-done.14
  156.1 1.0 copy-done.16
  157.2 1.0 copy-done.18
  160.3 8.6 %draft_logits.1 = (f32[1024,1024]{1,0:T(8,128)S(1)}, f32[8,1024]{1,0:T(8,128)S(1)}) custom-call(s32[16]{0:T(128)S(1)} %pad_add_fusion.place, bf16[4,32,2048]{2,1,0:T(8,128)(2,1)S(1)} %bitcast.104, bf16[4,32,2048]{2,1,0:T(8,128)(2,1)S(1)} %copy-done.14, bf16[4,32,2048]{2,1,0:T(8,128)(2,1)S(1)} %copy-done.16, ...), custom_call_target="tpu_custom_call" | custom-call | flops 4294967296 | bytes 12582912 | tf_op jit(solution)/shard_map/draft_logits/pallas_call | solution.py:177
  168.9 2.0 copy-done
  171.0 16.7 %teacher_logits.1 = (f32[1024,1024]{1,0:T(8,128)}, f32[4,1024]{1,0:T(4,128)S(1)}) custom-call(s32[16]{0:T(128)S(1)} %pad_add_fusion.place, bf16[4,4,16,2560]{3,2,1,0:T(8,128)(2,1)S(1)} %pad_maximum_fusion.refs_0_, bf16[4,4,16,2560]{3,2,1,0:T(8,128)(2,1)} %collective-permute-done.7.refs_1_, bf16[4,4,16,2560]{3,2,1,0:T(8,128)(2,1)} %collective-permute-done.8.refs_2_, ...), custom_call_target="tpu_custom_call" | custom-call | flops 8589934592 | bytes 20971520 | tf_op jit(solution)/shard_map/teacher_logits/pallas_call | solution.py:237
  188.6 2.4 collective-permute-start.29
  191.0 2.5 collective-permute-start.28
  193.8 1.1 collective-permute-done.28
  195.3 1.2 collective-permute-start.32
  196.4 2.0 collective-permute-start.31
  198.5 1.7 collective-permute-done.33
  201.5 9.0 %collective-permute-start.36 = (f32[4,1024]{1,0:T(4,128)S(1)}, f32[4,1024]{1,0:T(4,128)S(1)}, u32[]{:S(2)}, u32[]{:S(2)}) collective-permute-start(f32[4,1024]{1,0:T(4,128)S(1)} %get-tuple-element.32), channel_id=1, source_target_pairs={{0,16},{16,32},{32,48},{48,0},{1,17},{17,33},{33,49},{49,1},{2,18}... | collective-permute-start | bytes 49160 | tf_op jit(solution)/shard_map/ppermute | solution.py:25
  210.5 3.5 %collective-permute-start.35 = (f32[4,1024]{1,0:T(4,128)S(1)}, f32[4,1024]{1,0:T(4,128)S(1)}, u32[]{:S(2)}, u32[]{:S(2)}) collective-permute-start(f32[4,1024]{1,0:T(4,128)S(1)} %get-tuple-element.32), channel_id=1, source_target_pairs={{0,32},{16,48},{32,0},{48,16},{1,33},{17,49},{33,1},{49,17},{2,34}... | collective-permute-start | bytes 49160 | tf_op jit(solution)/shard_map/ppermute | solution.py:25
  214.0 2.5 collective-permute-start.34
  216.7 1.3 collective-permute-done.34
  218.3 2.2 copy-done.1
  220.5 1.6 copy-done.5
  222.1 8.8 %gradient_parts.1 = bf16[8,8,4,32,256]{4,3,2,1,0:T(8,128)(2,1)S(1)} custom-call(s32[2]{0:T(128)S(1)} %add_multiply_fusion.starts, f32[1024,1024]{1,0:T(8,128)S(1)} %copy-done.1, f32[1024,1024]{1,0:T(8,128)} %copy-done, f32[8,1024]{1,0:T(8,128)S(1)} %stack.170.rows_ref, bf16[512,2048]{1,0:T(8,128)(2,1)S(1)} %copy-done.2, bf16[512,2048]{1,0:T(8,128)(2,1)S(1)} %copy-done.5), custom_call_target="tpu_custom_call" | custom-call | flops 4294967296 | bytes 16777216 | tf_op jit(solution)/shard_map/gradient_parts/pallas_call | solution.py:286
  230.9 44.9 %all_to_all.15 = bf16[64,128,256]{2,1,0:T(8,128)(2,1)S(1)} all-to-all(bf16[64,128,256]{2,1,0:T(8,128)(2,1)S(1)} %bitcast.98), channel_id=1, replica_groups=mesh['yh'=2,'z'=4,'c'=2,'x'=4,'yl'=2] {'yh','z','x','yl'}, dimensions={0} | all-to-all | bytes 8388608 | tf_op jit(solution)/shard_map/all_to_all | solution.py:522
  275.8 1.2 convert_reduce_fusion
  (141 shorter events, 24.0 us)
Async XLA Ops:
  0.0 13.8 %copy-start.26 = (s32[32]{0:T(128)S(1)}, s32[32]{0:T(128)}, u32[]{:S(2)}) copy-start(s32[32]{0:T(128)} %param.25) | copy-start | bytes 388
  5.6 11.3 %copy-start.27 = (s32[4]{0:T(128)S(1)}, s32[4]{0:T(128)}, u32[]{:S(2)}) copy-start(s32[4]{0:T(128)} %param.24) | copy-start | bytes 52
  5.7 19.1 %all-to-all-start = ((bf16[8,128,256]{2,1,0:T(8,128)(2,1)}), bf16[8,128,256]{2,1,0:T(8,128)(2,1)S(1)}, u32[]{:S(2)}, u32[]{:S(2)}) async-start(bf16[8,128,256]{2,1,0:T(8,128)(2,1)} %get-tuple-element.11), calls=%async_computation | async-start | bytes 1048576 | tf_op jit(solution)/shard_map/all_to_all | solution.py:402
  24.8 1.9 collective-permute-start
  28.5 2.2 copy-start.23
  29.7 7.2 %copy-start.11 = (bf16[128,2048]{1,0:T(8,128)(2,1)S(1)}, bf16[128,2048]{1,0:T(8,128)(2,1)}, u32[]{:S(2)}) copy-start(bf16[128,2048]{1,0:T(8,128)(2,1)} %param.21) | copy-start | bytes 1572868
  30.7 25.3 %copy-start.24 = (f32[4096]{0:T(1024)S(1)}, f32[4096]{0:T(1024)}, u32[]{:S(2)}) copy-start(f32[4096]{0:T(1024)} %param.19) | copy-start | bytes 49156
  30.7 34.2 %copy-start.2 = (bf16[512,2048]{1,0:T(8,128)(2,1)S(1)}, bf16[512,2048]{1,0:T(8,128)(2,1)}, u32[]{:S(2)}) copy-start(bf16[512,2048]{1,0:T(8,128)(2,1)} %own_ref.1) | copy-start | bytes 6291460
  32.5 21.1 %all-to-all-start.1 = ((bf16[8,16,4096]{2,1,0:T(8,128)(2,1)}), bf16[8,16,4096]{2,1,0:T(8,128)(2,1)}, u32[]{:S(2)}, u32[]{:S(2)}) async-start(bf16[8,16,4096]{2,1,0:T(8,128)(2,1)} %bitcast.105), calls=%async_computation.1 | async-start | bytes 2097152 | tf_op jit(solution)/shard_map/all_to_all | solution.py:442
  36.9 20.5 %collective-permute-start.20 = (bf16[4,32,2048]{2,1,0:T(8,128)(2,1)S(1)}, bf16[4,32,2048]{2,1,0:T(8,128)(2,1)S(1)}, u32[]{:S(2)}, u32[]{:S(2)}) collective-permute-start(bf16[4,32,2048]{2,1,0:T(8,128)(2,1)S(1)} %bitcast.101), channel_id=1, source_target_pairs={{0,48},{16,0},{32,16},{48,32},{1,49},{17,1},{33,17},{49,33},{2,50}... | collective-permute-start | bytes 1572872 | tf_op jit(solution)/shard_map/ppermute | solution.py:25
  38.1 30.4 %collective-permute-start.22 = (bf16[4,32,2048]{2,1,0:T(8,128)(2,1)S(1)}, bf16[4,32,2048]{2,1,0:T(8,128)(2,1)}, u32[]{:S(2)}, u32[]{:S(2)}) collective-permute-start(bf16[4,32,2048]{2,1,0:T(8,128)(2,1)S(1)} %bitcast.102), channel_id=1, source_target_pairs={{0,16},{16,32},{32,48},{48,0},{1,17},{17,33},{33,49},{49,1},{2,18}... | collective-permute-start | bytes 1572872 | tf_op jit(solution)/shard_map/ppermute | solution.py:25
  39.0 23.9 %collective-permute-start.23 = (bf16[4,32,2048]{2,1,0:T(8,128)(2,1)S(1)}, bf16[4,32,2048]{2,1,0:T(8,128)(2,1)}, u32[]{:S(2)}, u32[]{:S(2)}) collective-permute-start(bf16[4,32,2048]{2,1,0:T(8,128)(2,1)S(1)} %bitcast.103), channel_id=1, source_target_pairs={{0,64},{64,0},{1,65},{65,1},{2,66},{66,2},{3,67},{67,3},{4,68},{68... | collective-permute-start | bytes 1572872 | tf_op jit(solution)/shard_map/ppermute | solution.py:25
  40.7 130.2 %collective-permute-start.19 = (bf16[512,4096]{1,0:T(8,128)(2,1)}, bf16[512,4096]{1,0:T(8,128)(2,1)}, u32[]{:S(2)}, u32[]{:S(2)}) collective-permute-start(bf16[512,4096]{1,0:T(8,128)(2,1)} %refs_8_.3), channel_id=1, source_target_pairs={{0,8},{8,0},{1,9},{9,1},{2,10},{10,2},{3,11},{11,3},{4,12},{12,4},... | collective-permute-start | bytes 12582920 | tf_op jit(solution)/shard_map/ppermute | solution.py:25
  57.0 7.9 %collective-permute-start.12 = (bf16[16,1536]{1,0:T(8,128)(2,1)S(1)}, bf16[16,1536]{1,0:T(8,128)(2,1)S(1)}, u32[]{:S(2)}, u32[]{:S(2)}) collective-permute-start(bf16[16,1536]{1,0:T(8,128)(2,1)S(1)} %get-tuple-element.28), channel_id=1, source_target_pairs={{0,2},{1,3},{2,4},{3,5},{4,6},{5,7},{6,0},{7,1},{8,9},{9,72},{10,1... | collective-permute-start | bytes 147464 | tf_op jit(solution)/shard_map/ppermute | solution.py:46
  57.4 66.8 %copy-start.13 = (bf16[4,32,2048]{2,1,0:T(8,128)(2,1)}, bf16[4,32,2048]{2,1,0:T(8,128)(2,1)S(1)}, u32[]{:S(2)}) copy-start(bf16[4,32,2048]{2,1,0:T(8,128)(2,1)S(1)} %collective-permute-done.20.refs_1_) | copy-start | bytes 1572868
  57.4 7.5 %collective-permute-start.11 = (bf16[16,1536]{1,0:T(8,128)(2,1)S(1)}, bf16[16,1536]{1,0:T(8,128)(2,1)S(1)}, u32[]{:S(2)}, u32[]{:S(2)}) collective-permute-start(bf16[16,1536]{1,0:T(8,128)(2,1)S(1)} %get-tuple-element.28), channel_id=1, source_target_pairs={{0,4},{1,5},{2,6},{3,7},{4,0},{5,1},{6,2},{7,3},{8,72},{9,73},{10,... | collective-permute-start | bytes 147464 | tf_op jit(solution)/shard_map/ppermute | solution.py:46
  62.9 4.1 %collective-permute-start.10 = (bf16[16,1536]{1,0:T(8,128)(2,1)S(1)}, bf16[16,1536]{1,0:T(8,128)(2,1)S(1)}, u32[]{:S(2)}, u32[]{:S(2)}) collective-permute-start(bf16[16,1536]{1,0:T(8,128)(2,1)S(1)} %get-tuple-element.28), channel_id=1, source_target_pairs={{0,6},{1,7},{2,0},{3,1},{4,2},{5,3},{6,4},{7,5},{8,73},{9,8},{10,7... | collective-permute-start | bytes 147464 | tf_op jit(solution)/shard_map/ppermute | solution.py:46
  64.9 68.9 %collective-permute-start.27 = (bf16[512,2048]{1,0:T(8,128)(2,1)S(1)}, bf16[512,2048]{1,0:T(8,128)(2,1)S(1)}, u32[]{:S(2)}, u32[]{:S(2)}) collective-permute-start(bf16[512,2048]{1,0:T(8,128)(2,1)S(1)} %copy-done.2), channel_id=1, source_target_pairs={{0,8},{8,0},{1,9},{9,1},{2,10},{10,2},{3,11},{11,3},{4,12},{12,4},... | collective-permute-start | bytes 6291464 | tf_op jit(solution)/shard_map/ppermute | solution.py:25
  64.9 14.9 %collective-permute-start.21 = (bf16[4,32,2048]{2,1,0:T(8,128)(2,1)S(1)}, bf16[4,32,2048]{2,1,0:T(8,128)(2,1)S(1)}, u32[]{:S(2)}, u32[]{:S(2)}) collective-permute-start(bf16[4,32,2048]{2,1,0:T(8,128)(2,1)S(1)} %collective-permute-done.20.refs_1_), channel_id=1, source_target_pairs={{0,48},{16,0},{32,16},{48,32},{1,49},{17,1},{33,17},{49,33},{2,50}... | collective-permute-start | bytes 1572872 | tf_op jit(solution)/shard_map/ppermute | solution.py:25
  67.0 23.5 %collective-permute-start.24 = (bf16[4,32,2048]{2,1,0:T(8,128)(2,1)}, bf16[4,32,2048]{2,1,0:T(8,128)(2,1)S(1)}, u32[]{:S(2)}, u32[]{:S(2)}) collective-permute-start(bf16[4,32,2048]{2,1,0:T(8,128)(2,1)} %collective-permute-done.23.refs_4_), channel_id=1, source_target_pairs={{0,48},{16,0},{32,16},{48,32},{1,49},{17,1},{33,17},{49,33},{2,50}... | collective-permute-start | bytes 1572872 | tf_op jit(solution)/shard_map/ppermute | solution.py:25
  68.5 31.5 %collective-permute-start.15 = (bf16[4,16,1536]{2,1,0:T(8,128)(2,1)S(1)}, bf16[4,16,1536]{2,1,0:T(8,128)(2,1)S(1)}, u32[]{:S(2)}, u32[]{:S(2)}) collective-permute-start(bf16[4,16,1536]{2,1,0:T(8,128)(2,1)S(1)} %get-tuple-element.26), channel_id=1, source_target_pairs={{0,1},{1,64},{2,3},{3,66},{4,5},{5,68},{6,7},{7,70},{8,10},{9,11},... | collective-permute-start | bytes 589832 | tf_op jit(solution)/shard_map/ppermute | solution.py:46
  80.6 11.9 %collective-permute-start.3 = (bf16[16,2560]{1,0:T(8,128)(2,1)S(1)}, bf16[16,2560]{1,0:T(8,128)(2,1)S(1)}, u32[]{:S(2)}, u32[]{:S(2)}) collective-permute-start(bf16[16,2560]{1,0:T(8,128)(2,1)S(1)} %get-tuple-element.30), channel_id=1, source_target_pairs={{0,16},{1,17},{2,18},{3,19},{4,20},{5,21},{6,22},{7,23},{8,24},{9,... | collective-permute-start | bytes 245768 | tf_op jit(solution)/shard_map/ppermute | solution.py:46
  91.3 5.9 %collective-permute-start.2 = (bf16[16,2560]{1,0:T(8,128)(2,1)S(1)}, bf16[16,2560]{1,0:T(8,128)(2,1)S(1)}, u32[]{:S(2)}, u32[]{:S(2)}) collective-permute-start(bf16[16,2560]{1,0:T(8,128)(2,1)S(1)} %get-tuple-element.30), channel_id=1, source_target_pairs={{0,32},{1,33},{2,34},{3,35},{4,36},{5,37},{6,38},{7,39},{8,40},{9,... | collective-permute-start | bytes 245768 | tf_op jit(solution)/shard_map/ppermute | solution.py:46
  92.5 6.0 %collective-permute-start.1 = (bf16[16,2560]{1,0:T(8,128)(2,1)S(1)}, bf16[16,2560]{1,0:T(8,128)(2,1)S(1)}, u32[]{:S(2)}, u32[]{:S(2)}) collective-permute-start(bf16[16,2560]{1,0:T(8,128)(2,1)S(1)} %get-tuple-element.30), channel_id=1, source_target_pairs={{0,48},{1,49},{2,50},{3,51},{4,52},{5,53},{6,54},{7,55},{8,56},{9,... | collective-permute-start | bytes 245768 | tf_op jit(solution)/shard_map/ppermute | solution.py:46
  97.2 13.8 %collective-permute-start.25 = (bf16[4,32,2048]{2,1,0:T(8,128)(2,1)}, bf16[4,32,2048]{2,1,0:T(8,128)(2,1)S(1)}, u32[]{:S(2)}, u32[]{:S(2)}) collective-permute-start(bf16[4,32,2048]{2,1,0:T(8,128)(2,1)} %collective-permute-done.23.refs_4_), channel_id=1, source_target_pairs={{0,16},{16,32},{32,48},{48,0},{1,17},{17,33},{33,49},{49,1},{2,18}... | collective-permute-start | bytes 1572872 | tf_op jit(solution)/shard_map/ppermute | solution.py:25
  98.5 7.2 %collective-permute-start.14 = (bf16[4,16,1536]{2,1,0:T(8,128)(2,1)S(1)}, bf16[4,16,1536]{2,1,0:T(8,128)(2,1)S(1)}, u32[]{:S(2)}, u32[]{:S(2)}) collective-permute-start(bf16[4,16,1536]{2,1,0:T(8,128)(2,1)S(1)} %get-tuple-element.26), channel_id=1, source_target_pairs={{0,64},{1,65},{2,66},{3,67},{4,68},{5,69},{6,70},{7,71},{8,12},{9,... | collective-permute-start | bytes 589832 | tf_op jit(solution)/shard_map/ppermute | solution.py:46
  100.0 7.9 %collective-permute-start.13 = (bf16[4,16,1536]{2,1,0:T(8,128)(2,1)S(1)}, bf16[4,16,1536]{2,1,0:T(8,128)(2,1)S(1)}, u32[]{:S(2)}, u32[]{:S(2)}) collective-permute-start(bf16[4,16,1536]{2,1,0:T(8,128)(2,1)S(1)} %get-tuple-element.26), channel_id=1, source_target_pairs={{0,65},{1,0},{2,67},{3,2},{4,69},{5,4},{6,71},{7,6},{8,14},{9,15},... | collective-permute-start | bytes 589832 | tf_op jit(solution)/shard_map/ppermute | solution.py:46
  105.6 8.3 %collective-permute-start.6 = (bf16[4,16,2560]{2,1,0:T(8,128)(2,1)S(1)}, bf16[4,16,2560]{2,1,0:T(8,128)(2,1)S(1)}, u32[]{:S(2)}, u32[]{:S(2)}) collective-permute-start(bf16[4,16,2560]{2,1,0:T(8,128)(2,1)S(1)} %get-tuple-element.22), channel_id=1, source_target_pairs={{0,1},{1,64},{2,3},{3,66},{4,5},{5,68},{6,7},{7,70},{8,10},{9,11},... | collective-permute-start | bytes 983048 | tf_op jit(solution)/shard_map/ppermute | solution.py:46
  107.9 10.7 %collective-permute-start.5 = (bf16[4,16,2560]{2,1,0:T(8,128)(2,1)S(1)}, bf16[4,16,2560]{2,1,0:T(8,128)(2,1)S(1)}, u32[]{:S(2)}, u32[]{:S(2)}) collective-permute-start(bf16[4,16,2560]{2,1,0:T(8,128)(2,1)S(1)} %get-tuple-element.22), channel_id=1, source_target_pairs={{0,64},{1,65},{2,66},{3,67},{4,68},{5,69},{6,70},{7,71},{8,12},{9,... | collective-permute-start | bytes 983048 | tf_op jit(solution)/shard_map/ppermute | solution.py:46
  111.0 36.8 %copy-start.19 = (bf16[4,32,2048]{2,1,0:T(8,128)(2,1)}, bf16[4,32,2048]{2,1,0:T(8,128)(2,1)S(1)}, u32[]{:S(2)}) copy-start(bf16[4,32,2048]{2,1,0:T(8,128)(2,1)S(1)} %collective-permute-done.25.refs_7_) | copy-start | bytes 1572868
  111.0 33.5 %collective-permute-start.16 = (bf16[4,4,16,1536]{3,2,1,0:T(8,128)(2,1)}, bf16[4,4,16,1536]{3,2,1,0:T(8,128)(2,1)S(1)}, u32[]{:S(2)}, u32[]{:S(2)}) collective-permute-start(bf16[4,4,16,1536]{3,2,1,0:T(8,128)(2,1)} %pad_maximum_fusion.1.refs_4_), channel_id=1, source_target_pairs={{0,48},{1,49},{2,50},{3,51},{4,52},{5,53},{6,54},{7,55},{8,56},{9,... | collective-permute-start | bytes 2359304 | tf_op jit(solution)/shard_map/ppermute | solution.py:46
  113.9 7.1 %collective-permute-start.4 = (bf16[4,16,2560]{2,1,0:T(8,128)(2,1)S(1)}, bf16[4,16,2560]{2,1,0:T(8,128)(2,1)S(1)}, u32[]{:S(2)}, u32[]{:S(2)}) collective-permute-start(bf16[4,16,2560]{2,1,0:T(8,128)(2,1)S(1)} %get-tuple-element.22), channel_id=1, source_target_pairs={{0,65},{1,0},{2,67},{3,2},{4,69},{5,4},{6,71},{7,6},{8,14},{9,15},... | collective-permute-start | bytes 983048 | tf_op jit(solution)/shard_map/ppermute | solution.py:46
  118.5 14.3 %collective-permute-start.26 = (bf16[4,32,2048]{2,1,0:T(8,128)(2,1)S(1)}, bf16[4,32,2048]{2,1,0:T(8,128)(2,1)S(1)}, u32[]{:S(2)}, u32[]{:S(2)}) collective-permute-start(bf16[4,32,2048]{2,1,0:T(8,128)(2,1)S(1)} %collective-permute-done.25.refs_7_), channel_id=1, source_target_pairs={{0,16},{16,32},{32,48},{48,0},{1,17},{17,33},{33,49},{49,1},{2,18}... | collective-permute-start | bytes 1572872 | tf_op jit(solution)/shard_map/ppermute | solution.py:25
  121.0 26.8 %collective-permute-start.17 = (bf16[4,4,16,1536]{3,2,1,0:T(8,128)(2,1)}, bf16[4,4,16,1536]{3,2,1,0:T(8,128)(2,1)S(1)}, u32[]{:S(2)}, u32[]{:S(2)}) collective-permute-start(bf16[4,4,16,1536]{3,2,1,0:T(8,128)(2,1)} %pad_maximum_fusion.1.refs_4_), channel_id=1, source_target_pairs={{0,32},{1,33},{2,34},{3,35},{4,36},{5,37},{6,38},{7,39},{8,40},{9,... | collective-permute-start | bytes 2359304 | tf_op jit(solution)/shard_map/ppermute | solution.py:46
  132.9 0.8 copy-start.21
  133.7 37.2 %collective-permute-start.7 = (bf16[4,4,16,2560]{3,2,1,0:T(8,128)(2,1)S(1)}, bf16[4,4,16,2560]{3,2,1,0:T(8,128)(2,1)}, u32[]{:S(2)}, u32[]{:S(2)}) collective-permute-start(bf16[4,4,16,2560]{3,2,1,0:T(8,128)(2,1)S(1)} %pad_maximum_fusion.refs_0_), channel_id=1, source_target_pairs={{0,6},{1,7},{2,0},{3,1},{4,2},{5,3},{6,4},{7,5},{8,73},{9,8},{10,7... | collective-permute-start | bytes 3932168 | tf_op jit(solution)/shard_map/ppermute | solution.py:46
  133.8 1.3 copy-start.3
  135.1 35.9 %collective-permute-start.8 = (bf16[4,4,16,2560]{3,2,1,0:T(8,128)(2,1)S(1)}, bf16[4,4,16,2560]{3,2,1,0:T(8,128)(2,1)}, u32[]{:S(2)}, u32[]{:S(2)}) collective-permute-start(bf16[4,4,16,2560]{3,2,1,0:T(8,128)(2,1)S(1)} %pad_maximum_fusion.refs_0_), channel_id=1, source_target_pairs={{0,4},{1,5},{2,6},{3,7},{4,0},{5,1},{6,2},{7,3},{8,72},{9,73},{10,... | collective-permute-start | bytes 3932168 | tf_op jit(solution)/shard_map/ppermute | solution.py:46
  144.4 0.9 copy-start.7
  145.3 25.6 %collective-permute-start.9 = (bf16[4,4,16,2560]{3,2,1,0:T(8,128)(2,1)S(1)}, bf16[4,4,16,2560]{3,2,1,0:T(8,128)(2,1)}, u32[]{:S(2)}, u32[]{:S(2)}) collective-permute-start(bf16[4,4,16,2560]{3,2,1,0:T(8,128)(2,1)S(1)} %pad_maximum_fusion.refs_0_), channel_id=1, source_target_pairs={{0,2},{1,3},{2,4},{3,5},{4,6},{5,7},{6,0},{7,1},{8,9},{9,72},{10,1... | collective-permute-start | bytes 3932168 | tf_op jit(solution)/shard_map/ppermute | solution.py:46
  147.8 0.9 copy-start.9
  148.7 22.2 %collective-permute-start.18 = (bf16[4,4,16,1536]{3,2,1,0:T(8,128)(2,1)}, bf16[4,4,16,1536]{3,2,1,0:T(8,128)(2,1)}, u32[]{:S(2)}, u32[]{:S(2)}) collective-permute-start(bf16[4,4,16,1536]{3,2,1,0:T(8,128)(2,1)} %pad_maximum_fusion.1.refs_4_), channel_id=1, source_target_pairs={{0,16},{1,17},{2,18},{3,19},{4,20},{5,21},{6,22},{7,23},{8,24},{9,... | collective-permute-start | bytes 2359304 | tf_op jit(solution)/shard_map/ppermute | solution.py:46
  152.4 1.6 copy-start.4
  154.0 1.0 copy-start.12
  155.1 1.0 copy-start.14
  156.1 1.0 copy-start.16
  157.2 1.0 copy-start.18
  158.2 1.0 copy-start.20
  159.3 1.0 copy-start.22
  160.3 10.7 %copy-start.8 = (bf16[4,4,16,1536]{3,2,1,0:T(8,128)(2,1)S(1)}, bf16[4,4,16,1536]{3,2,1,0:T(8,128)(2,1)}, u32[]{:S(2)}) copy-start(bf16[4,4,16,1536]{3,2,1,0:T(8,128)(2,1)} %copy-done.7) | copy-start | bytes 2359300
  160.3 10.7 %copy-start.10 = (bf16[4,4,16,1536]{3,2,1,0:T(8,128)(2,1)S(1)}, bf16[4,4,16,1536]{3,2,1,0:T(8,128)(2,1)}, u32[]{:S(2)}) copy-start(bf16[4,4,16,1536]{3,2,1,0:T(8,128)(2,1)} %copy-done.9) | copy-start | bytes 2359300
  168.9 2.0 copy-start
  171.0 22.5 %copy-start.25 = (s32[2048]{0:T(1024)S(1)}, s32[2048]{0:T(1024)}, u32[]{:S(2)}) copy-start(s32[2048]{0:T(1024)} %param.23) | copy-start | bytes 24580
  187.7 5.9 %collective-permute-start.30 = (f32[4,1024]{1,0:T(4,128)S(1)}, f32[4,1024]{1,0:T(4,128)S(1)}, u32[]{:S(2)}, u32[]{:S(2)}) collective-permute-start(f32[4,1024]{1,0:T(4,128)S(1)} %get-tuple-element.16), channel_id=1, source_target_pairs={{0,2},{2,4},{4,6},{6,0},{1,3},{3,5},{5,7},{7,1},{8,10},{10,12},{12... | collective-permute-start | bytes 49160 | tf_op jit(solution)/shard_map/ppermute | solution.py:25
  188.6 5.2 %collective-permute-start.29 = (f32[4,1024]{1,0:T(4,128)S(1)}, f32[4,1024]{1,0:T(4,128)S(1)}, u32[]{:S(2)}, u32[]{:S(2)}) collective-permute-start(f32[4,1024]{1,0:T(4,128)S(1)} %get-tuple-element.16), channel_id=1, source_target_pairs={{0,4},{2,6},{4,0},{6,2},{1,5},{3,7},{5,1},{7,3},{8,12},{10,14},{12... | collective-permute-start | bytes 49160 | tf_op jit(solution)/shard_map/ppermute | solution.py:25
  191.0 3.9 %collective-permute-start.28 = (f32[4,1024]{1,0:T(4,128)S(1)}, f32[4,1024]{1,0:T(4,128)S(1)}, u32[]{:S(2)}, u32[]{:S(2)}) collective-permute-start(f32[4,1024]{1,0:T(4,128)S(1)} %get-tuple-element.16), channel_id=1, source_target_pairs={{0,6},{2,0},{4,2},{6,4},{1,7},{3,1},{5,3},{7,5},{8,14},{10,8},{12,... | collective-permute-start | bytes 49160 | tf_op jit(solution)/shard_map/ppermute | solution.py:25
  195.2 5.0 %collective-permute-start.33 = (f32[4,1024]{1,0:T(4,128)S(1)}, f32[4,1024]{1,0:T(4,128)S(1)}, u32[]{:S(2)}, u32[]{:S(2)}) collective-permute-start(f32[4,1024]{1,0:T(4,128)S(1)} %get-tuple-element.34), channel_id=1, source_target_pairs={{0,1},{1,64},{64,65},{65,0},{2,3},{3,66},{66,67},{67,2},{4,5},{5,6... | collective-permute-start | bytes 49160 | tf_op jit(solution)/shard_map/ppermute | solution.py:25
  195.3 5.3 %collective-permute-start.32 = (f32[4,1024]{1,0:T(4,128)S(1)}, f32[4,1024]{1,0:T(4,128)S(1)}, u32[]{:S(2)}, u32[]{:S(2)}) collective-permute-start(f32[4,1024]{1,0:T(4,128)S(1)} %get-tuple-element.34), channel_id=1, source_target_pairs={{0,64},{1,65},{64,0},{65,1},{2,66},{3,67},{66,2},{67,3},{4,68},{5,... | collective-permute-start | bytes 49160 | tf_op jit(solution)/shard_map/ppermute | solution.py:25
  196.4 4.8 %collective-permute-start.31 = (f32[4,1024]{1,0:T(4,128)S(1)}, f32[4,1024]{1,0:T(4,128)S(1)}, u32[]{:S(2)}, u32[]{:S(2)}) collective-permute-start(f32[4,1024]{1,0:T(4,128)S(1)} %get-tuple-element.34), channel_id=1, source_target_pairs={{0,65},{1,0},{64,1},{65,64},{2,67},{3,2},{66,3},{67,66},{4,69},{5,... | collective-permute-start | bytes 49160 | tf_op jit(solution)/shard_map/ppermute | solution.py:25
  201.5 15.2 %collective-permute-start.36 = (f32[4,1024]{1,0:T(4,128)S(1)}, f32[4,1024]{1,0:T(4,128)S(1)}, u32[]{:S(2)}, u32[]{:S(2)}) collective-permute-start(f32[4,1024]{1,0:T(4,128)S(1)} %get-tuple-element.32), channel_id=1, source_target_pairs={{0,16},{16,32},{32,48},{48,0},{1,17},{17,33},{33,49},{49,1},{2,18}... | collective-permute-start | bytes 49160 | tf_op jit(solution)/shard_map/ppermute | solution.py:25
  210.5 6.2 %collective-permute-start.35 = (f32[4,1024]{1,0:T(4,128)S(1)}, f32[4,1024]{1,0:T(4,128)S(1)}, u32[]{:S(2)}, u32[]{:S(2)}) collective-permute-start(f32[4,1024]{1,0:T(4,128)S(1)} %get-tuple-element.32), channel_id=1, source_target_pairs={{0,32},{16,48},{32,0},{48,16},{1,33},{17,49},{33,1},{49,17},{2,34}... | collective-permute-start | bytes 49160 | tf_op jit(solution)/shard_map/ppermute | solution.py:25
  214.0 4.0 %collective-permute-start.34 = (f32[4,1024]{1,0:T(4,128)S(1)}, f32[4,1024]{1,0:T(4,128)S(1)}, u32[]{:S(2)}, u32[]{:S(2)}) collective-permute-start(f32[4,1024]{1,0:T(4,128)S(1)} %get-tuple-element.32), channel_id=1, source_target_pairs={{0,48},{16,0},{32,16},{48,32},{1,49},{17,1},{33,17},{49,33},{2,50}... | collective-permute-start | bytes 49160 | tf_op jit(solution)/shard_map/ppermute | solution.py:25
  218.3 2.2 copy-start.1
  220.5 1.6 copy-start.5
  (3 other events, 2.3 us)
